TPU v7x, 32 devices: a whole 2x2x4 slice. The times are simulated.
32 devices in a mesh: gx: 8 (over z, core), gy: 4 (over y, x).
Axes of the slice: x: 2, y: 2, z: 4, core: 2. Of those that a mesh axis runs over, the one named last changes fastest.
Arguments:
- mesh_state: bfloat16 [128, 128, 32, 128], P('gx', 'gy'), may hold values from -6 to 6
- part_feat: bfloat16 [131072, 128], P(('gx', 'gy')), may hold values from -6 to 6
- cell_index: int32 [131072], P(('gx', 'gy')), may hold values from 0 to 16383, as said below
- pairs: int32 [2, 786432], P(None, ('gx', 'gy')), may hold values from 0 to 4095, as said below
- dest: int32 [131072], P(('gx', 'gy')), may hold values from 0 to 8, as said below
- mass: float32 [131072], P(('gx', 'gy')), may hold values from 0.5 to 2
- velocity: float32 [3, 131072], P(None, ('gx', 'gy')), may hold values from -30 to 30
- w_enc: bfloat16 [128, 128], replicated, may hold values from -0.5 to 0.5
- w_mesh: bfloat16 [128, 128], replicated, may hold values from -0.21875 to 0.21875
- w_pair: bfloat16 [128, 256], replicated, may hold values from -0.5 to 0.5
- w_edge: bfloat16 [128, 128], replicated, may hold values from -0.5 to 0.5
- w_node: bfloat16 [256, 128], replicated, may hold values from -0.25 to 0.25
- w_accel: bfloat16 [3, 128], replicated, may hold values from -0.5 to 0.5
Outputs:
- mesh_out: bfloat16 [128, 128, 32, 128], P('gx', 'gy')
- stay_feat: bfloat16 [131072, 128], P(('gx', 'gy'))
- stay_vel: float32 [3, 131072], P(None, ('gx', 'gy'))
- arrived_feat: bfloat16 [32768, 128], P(('gx', 'gy'))
- arrived_vel: float32 [4, 32768], P(None, ('gx', 'gy'))
Inputs may be any that keep to these rules, and one draw needn't show every extreme that they name: `dest`: 0 means the particle stays; k from 1 to 8 moves it in the k-th direction of the steps. At most 128 particles of one device take any one direction, and some device receives 128 particles from each of its eight neighbours. `cell_index`: A device's particles come in 8 aligned groups of 512 rows; the particles of group g lie in cells g * 2048 to (g + 1) * 2048 - 1 of the device's block. `pairs`: A device's columns come in 8 aligned groups of 3072; both rows of a column of group g name particles of the device's group g, rows g * 512 to (g + 1) * 512 - 1.
All inputs are finite; a program needn't handle non-finite values.
Results may differ from a plain program's by a relative error of at most 0.0085.
Values may be sent and summed in bfloat16 or wider, within the bound.
A program may use at most 128 MiB of HBM per device.

v0:
```python
import functools
import jax
import jax.numpy as jnp
from jax import lax
from jax.experimental import pallas as pl
from jax.experimental.pallas import tpu as pltpu
from jax.sharding import PartitionSpec as P

directions = ((-1, -1), (-1, 0), (-1, 1), (0, -1), (0, 1), (1, -1), (1, 0), (1, 1))
LANES = 128
VMEM_LIMIT = 60 * 1024 * 1024


def from_behind(block, axis, distance):
    devices = range(lax.axis_size(axis))
    route = [((i - distance) % len(devices), i) for i in devices]
    return lax.ppermute(block, axis, route)


def summed_over(total, axis):
    devices = lax.axis_size(axis)
    if devices & (devices - 1):
        return lax.psum(total, axis)
    distance = 1
    while distance < devices:
        total = total + from_behind(total, axis, distance)
        distance *= 2
    return total


def group_sizes(parts, cells):
    members = min(512, parts)
    count = parts // members
    return (members, count, cells // count)


def silu(v):
    half = 0.5 * v
    return half + half * jnp.tanh(half)


def f32dot(a, b):
    return jnp.dot(a, b, preferred_element_type=jnp.float32)


def row_hot(keys, rows, first):
    lanes = lax.broadcasted_iota(jnp.int32, (rows, keys.shape[1]), 0) + first
    return jnp.where(lanes == keys, 1.0, 0.0).astype(jnp.bfloat16)


def col_hot(cols, start, stop, width):
    lanes = lax.broadcasted_iota(jnp.int32, (LANES, width), 1)
    parts = [
        jnp.where(lanes == cols[:, j : j + 1], 1.0, 0.0).astype(jnp.bfloat16)
        for j in range(start, stop)
    ]
    return jnp.concatenate(parts, axis=0)


def encode_kernel(chunk, cell_ref, feat_ref, state_ref, w_enc_ref, out_ref):
    span = state_ref.shape[0]
    base = pl.program_id(0) * span
    cells = cell_ref[0] - base

    def body(i, carry):
        first = pl.multiple_of(i * chunk, chunk)
        onehot = row_hot(cells, chunk, first)
        deposit = f32dot(onehot, feat_ref[...]).astype(jnp.bfloat16)
        rows = pl.ds(first, chunk)
        out_ref[rows, :] = (
            state_ref[rows, :].astype(jnp.float32) + f32dot(deposit, w_enc_ref[...])
        ).astype(jnp.bfloat16)
        return carry

    lax.fori_loop(0, span // chunk, body, 0)


def edge_kernel(
    members, send_ref, recv_ref, recv_row_ref, feat_ref, w_pair_ref, w_edge_ref, out_ref
):
    base = pl.program_id(0) * members
    width = feat_ref.shape[1]
    proj = f32dot(feat_ref[...], w_pair_ref[...]).astype(jnp.bfloat16)
    table = jnp.concatenate([proj[:, :width], proj[:, width:]], axis=0)
    send_cols = (send_ref[0] - base).T
    recv_cols = (recv_ref[0] - base).T
    turns = send_cols.shape[1]
    step = 6 if turns % 6 == 0 else 1
    total = jnp.zeros((members, width), jnp.float32)
    for start in range(0, turns, step):
        hot = jnp.concatenate(
            [
                col_hot(send_cols, start, start + step, members),
                col_hot(recv_cols, start, start + step, members),
            ],
            axis=1,
        )
        act = silu(f32dot(hot, table)).astype(jnp.bfloat16)
        keys = recv_row_ref[0, :, start * LANES : (start + step) * LANES] - base
        total = total + f32dot(row_hot(keys, members, 0), act)
    edge_sum = f32dot(total.astype(jnp.bfloat16), w_edge_ref[...])
    out_ref[...] = edge_sum.astype(jnp.bfloat16)


def node_kernel(
    plane,
    depth,
    cap,
    below_ref,
    centre_ref,
    above_ref,
    xlo_ref,
    xhi_ref,
    ylo_ref,
    yhi_ref,
    cell_ref,
    dest_ref,
    dest_row_ref,
    edge_ref,
    feat_ref,
    mass_ref,
    vel_ref,
    w_mesh_ref,
    w_node_ref,
    w_accel_ref,
    mesh_ref,
    stay_ref,
    vel1_ref,
    packed_ref,
    total_ref,
    slots_ref,
    carry_ref,
):
    step = pl.program_id(0)
    last = pl.num_programs(0) - 1
    span, width = centre_ref.shape
    members = feat_ref.shape[0]
    planes = span // plane
    base = step * span

    @pl.when(step == 0)
    def _():
        slots_ref[...] = jnp.zeros_like(slots_ref)
        carry_ref[...] = jnp.zeros_like(carry_ref)
        total_ref[...] = jnp.zeros_like(total_ref)

    level = lax.broadcasted_iota(jnp.int32, (plane, width), 0) % depth
    for p in range(planes):
        rows = slice(p * plane, (p + 1) * plane)
        centre = centre_ref[rows, :].astype(jnp.float32)
        if p == 0:
            below = jnp.where(
                step == 0, xlo_ref[...].astype(jnp.float32), below_ref[...].astype(jnp.float32)
            )
        else:
            below = centre_ref[(p - 1) * plane : p * plane, :].astype(jnp.float32)
        if p == planes - 1:
            above = jnp.where(
                step == last, xhi_ref[...].astype(jnp.float32), above_ref[...].astype(jnp.float32)
            )
        else:
            above = centre_ref[(p + 1) * plane : (p + 2) * plane, :].astype(jnp.float32)
        edge = slice(p * depth, (p + 1) * depth)
        left = jnp.concatenate([ylo_ref[edge, :].astype(jnp.float32), centre[:-depth]], axis=0)
        right = jnp.concatenate([centre[depth:], yhi_ref[edge, :].astype(jnp.float32)], axis=0)
        down = jnp.where(level == 0, 0.0, pltpu.roll(centre, 1, 0))
        up = jnp.where(level == depth - 1, 0.0, pltpu.roll(centre, plane - 1, 0))
        sides = (below + above + left + right + (up + down)).astype(jnp.bfloat16)
        mesh_ref[rows, :] = (centre + silu(f32dot(sides, w_mesh_ref[...]))).astype(jnp.bfloat16)

    cell_cols = (cell_ref[0] - base).T
    dest_cols = dest_ref[0].T
    turns = members // LANES
    near = f32dot(col_hot(cell_cols, 0, turns, span), mesh_ref[...]).astype(jnp.bfloat16)
    update = f32dot(edge_ref[...], w_node_ref[:width, :]) + f32dot(near, w_node_ref[width:, :])
    h_new = (feat_ref[...].astype(jnp.float32) + silu(update)).astype(jnp.bfloat16)
    h_wide = h_new.astype(jnp.float32)
    for j in range(turns):
        rows = slice(j * LANES, (j + 1) * LANES)
        stay_ref[rows, :] = jnp.where(dest_cols[:, j : j + 1] == 0, h_wide[rows], 0.0).astype(
            jnp.bfloat16
        )
    accel = lax.dot_general(
        w_accel_ref[...], h_new, (((1,), (1,)), ((), ())), preferred_element_type=jnp.float32
    )
    vel1 = vel_ref[...] + accel[:3]
    mass = mass_ref[0]
    vel1_ref[...] = vel1
    sums = jnp.concatenate([mass * vel1, mass], axis=0)
    total_ref[...] += sum(sums[:, j * LANES : (j + 1) * LANES] for j in range(turns))

    dest = dest_row_ref[0]
    ways = lax.broadcasted_iota(jnp.int32, (8, members), 0) + 1
    chosen_way = jnp.where(ways == dest, 1.0, 0.0)
    earlier = jnp.where(
        lax.broadcasted_iota(jnp.int32, (members, members), 0)
        < lax.broadcasted_iota(jnp.int32, (members, members), 1),
        1.0,
        0.0,
    ).astype(jnp.bfloat16)
    place = f32dot(chosen_way.astype(jnp.bfloat16), earlier) + carry_ref[:, :1]
    slot = jnp.sum(place * chosen_way, axis=0, keepdims=True).astype(jnp.int32)
    carry_ref[...] += jnp.sum(chosen_way, axis=1, keepdims=True)
    key = jnp.where(dest > 0, (dest - 1) * cap + slot, -1)
    extra = jnp.concatenate([vel1, mass, jnp.zeros((LANES - 4, members), jnp.float32)], axis=0)
    values = jnp.concatenate([h_new, extra.T.astype(jnp.bfloat16)], axis=1)
    half = slots_ref.shape[0] // 2
    for first in (0, half):
        rows = slice(first, first + half)
        slots_ref[rows, :] += f32dot(row_hot(key, half, first), values)

    @pl.when(step == last)
    def _():
        moving = slots_ref[:, width:].T
        for k in range(8):
            rows = slice(k * cap, (k + 1) * cap)
            packed_ref[k, :cap, :] = slots_ref[rows, :width].astype(jnp.bfloat16)
            packed_ref[k, cap:, :] = moving[:16, rows].astype(jnp.bfloat16)


def unpack(moving, drift):
    values = moving.astype(jnp.float32)
    weight = values[..., 3:4, :]
    speed = jnp.where(weight > 0, values[..., :3, :] - drift[:, None], 0.0)
    return jnp.concatenate([speed, weight], axis=-2)


def whole(shape):
    return pl.BlockSpec(shape, lambda g: (0,) * len(shape))


def shards(
    mesh_state,
    part_feat,
    cell_index,
    pairs,
    dest,
    mass,
    velocity,
    w_enc,
    w_mesh,
    w_pair,
    w_edge,
    w_node,
    w_accel,
):
    shape = mesh_state.shape
    parts, width = part_feat.shape
    cx, cy, cz, channels = shape
    cells = cx * cy * cz
    plane = cy * cz
    members, count, span = group_sizes(parts, cells)
    planes = span // plane
    per_group = pairs.shape[1] // count
    cap = parts // 32
    bf16, f32 = (jnp.bfloat16, jnp.float32)
    params = pltpu.CompilerParams(vmem_limit_bytes=VMEM_LIMIT)

    by_rows = pl.BlockSpec((members, width), lambda g: (g, 0))
    by_cells = pl.BlockSpec((span, channels), lambda g: (g, 0))
    by_row = pl.BlockSpec((1, 1, members), lambda g: (g, 0, 0))
    by_tile = pl.BlockSpec((1, members // LANES, LANES), lambda g: (g, 0, 0))

    cell_row = cell_index.reshape(count, 1, members)
    cell_tile = cell_index.reshape(count, members // LANES, LANES)
    dest_row = dest.reshape(count, 1, members)
    dest_tile = dest.reshape(count, members // LANES, LANES)
    mass_row = mass.reshape(count, 1, members)
    send_tile = pairs[0].reshape(count, per_group // LANES, LANES)
    recv_tile = pairs[1].reshape(count, per_group // LANES, LANES)
    recv_row = pairs[1].reshape(count, 1, per_group)
    accel8 = jnp.pad(w_accel, ((0, 8 - w_accel.shape[0]), (0, 0)))

    mesh1 = pl.pallas_call(
        functools.partial(encode_kernel, min(512, span)),
        grid=(count,),
        out_shape=jax.ShapeDtypeStruct((cells, channels), bf16),
        in_specs=[by_row, by_rows, by_cells, whole(w_enc.shape)],
        out_specs=by_cells,
        compiler_params=params,
        cost_estimate=pl.CostEstimate(
            flops=2 * cells * members * width, bytes_accessed=4 * cells * channels, transcendentals=0
        ),
        name="encode",
    )(cell_row, part_feat, mesh_state.reshape(cells, channels), w_enc)

    grid1 = mesh1.reshape(shape)
    xlo = from_behind(grid1[cx - 1 :].reshape(plane, channels), "gx", 1)
    xhi = from_behind(grid1[:1].reshape(plane, channels), "gx", -1)
    ylo = from_behind(grid1[:, cy - 1 :].reshape(cx * cz, channels), "gy", 1)
    yhi = from_behind(grid1[:, :1].reshape(cx * cz, channels), "gy", -1)

    by_pairs = pl.BlockSpec((1, per_group // LANES, LANES), lambda g: (g, 0, 0))
    edge_sum = pl.pallas_call(
        functools.partial(edge_kernel, members),
        grid=(count,),
        out_shape=jax.ShapeDtypeStruct((parts, width), bf16),
        in_specs=[
            by_pairs,
            by_pairs,
            pl.BlockSpec((1, 1, per_group), lambda g: (g, 0, 0)),
            by_rows,
            whole(w_pair.shape),
            whole(w_edge.shape),
        ],
        out_specs=by_rows,
        compiler_params=params,
        cost_estimate=pl.CostEstimate(
            flops=6 * pairs.shape[1] * members * width,
            bytes_accessed=4 * parts * width,
            transcendentals=pairs.shape[1] * width,
        ),
        name="edges",
    )(send_tile, recv_tile, recv_row, part_feat, w_pair, w_edge)

    one_plane = lambda f: pl.BlockSpec((plane, channels), f)
    by_layer = pl.BlockSpec((planes * cz, channels), lambda g: (g, 0))
    by_speed = pl.BlockSpec((3, members), lambda g: (0, g))
    mesh2, stay_feat, vel1, packed, totals = pl.pallas_call(
        functools.partial(node_kernel, plane, cz, cap),
        grid=(count,),
        out_shape=(
            jax.ShapeDtypeStruct((cells, channels), bf16),
            jax.ShapeDtypeStruct((parts, width), bf16),
            jax.ShapeDtypeStruct((3, parts), f32),
            jax.ShapeDtypeStruct((8, cap + 16, width), bf16),
            jax.ShapeDtypeStruct((4, LANES), f32),
        ),
        in_specs=[
            one_plane(lambda g: (jnp.maximum(g * planes - 1, 0), 0)),
            by_cells,
            one_plane(lambda g: (jnp.minimum(g * planes + planes, cx - 1), 0)),
            whole((plane, channels)),
            whole((plane, channels)),
            by_layer,
            by_layer,
            by_tile,
            by_tile,
            by_row,
            by_rows,
            by_rows,
            by_row,
            by_speed,
            whole(w_mesh.shape),
            whole(w_node.shape),
            whole(accel8.shape),
        ],
        out_specs=(
            by_cells,
            by_rows,
            by_speed,
            whole((8, cap + 16, width)),
            whole((4, LANES)),
        ),
        scratch_shapes=[
            pltpu.VMEM((8 * cap, width + LANES), f32),
            pltpu.VMEM((8, LANES), f32),
        ],
        compiler_params=params,
        name="nodes",
    )(
        mesh1,
        mesh1,
        mesh1,
        xlo,
        xhi,
        ylo,
        yhi,
        cell_tile,
        dest_tile,
        dest_row,
        edge_sum,
        part_feat,
        mass_row,
        velocity,
        w_mesh,
        w_node,
        accel8,
    )

    sums = jnp.sum(summed_over(summed_over(totals, "gx"), "gy"), axis=1)
    drift = sums[:3] / sums[3]
    stay_vel = jnp.where((dest == 0)[None, :], vel1 - drift[:, None], 0.0)

    got = [packed[k] for k in range(8)]
    for axis, part in (("gx", 0), ("gy", 1)):
        for distance in (1, -1):
            chosen = [k for k, offset in enumerate(directions) if offset[part] == distance]
            moved = from_behind(jnp.stack([got[k] for k in chosen], axis=0), axis, distance)
            for place, k in enumerate(chosen):
                got[k] = moved[place]
    arrived = jnp.stack(got, axis=0)
    arrived_feat = arrived[:, :cap].reshape(-1, width)
    arrived_vel = unpack(arrived[:, cap : cap + 4], drift).transpose(1, 0, 2).reshape(4, -1)
    return (mesh2.reshape(shape), stay_feat, stay_vel, arrived_feat, arrived_vel)


def solution(mesh):
    placed = (
        P("gx", "gy", None, None),
        P(("gx", "gy"), None),
        P(("gx", "gy")),
        P(None, ("gx", "gy")),
        P(("gx", "gy")),
        P(("gx", "gy")),
        P(None, ("gx", "gy")),
        P(),
        P(),
        P(),
        P(),
        P(),
        P(),
    )
    return jax.shard_map(
        shards,
        mesh=mesh,
        in_specs=placed,
        out_specs=(
            P("gx", "gy", None, None),
            P(("gx", "gy"), None),
            P(None, ("gx", "gy")),
            P(("gx", "gy"), None),
            P(None, ("gx", "gy")),
        ),
        check_vma=False,
    )
```

profile of v0, /device:TPU:0, one launch (start us, length us, event | category | flops | bytes accessed | tf_op | source)
XLA Modules:
  0.0 127.4 jit_solution(14718468751108511670)
XLA Ops:
  0.6 17.0 %encode.1.below_ref.centre_ref.above_ref = bf16[16384,128]{1,0:T(8,128)(2,1)} custom-call(s32[8,1,512]{2,1,0:T(1,128)} %bitcast.36, bf16[4096,128]{1,0:T(8,128)(2,1)} %feat_ref.5, bf16[16384,128]{1,0:T(8,128)(2,1)} %bitcast.27, bf16[128,128]{1,0:T(8,128)(2,1)} %w_enc_ref.1), custom_call_target="tpu_custom_call" | custom-call | flops 2147483648 | bytes 8388608 | tf_op jit(solution)/shard_map/encode/pallas_call | solution.py:274
  17.6 1.1 fusion.2
  19.2 4.1 %collective-permute-start.1 = (bf16[1024,128]{1,0:T(8,128)(2,1)S(1)}, bf16[1024,128]{1,0:T(8,128)(2,1)S(1)}, u32[]{:S(2)}, u32[]{:S(2)}) collective-permute-start(bf16[1024,128]{1,0:T(8,128)(2,1)S(1)} %get-tuple-element.17), channel_id=1, source_target_pairs={{4,0},{8,4},{12,8},{16,12},{20,16},{24,20},{28,24},{0,28},{5,1},{9... | collective-permute-start | bytes 786440 | tf_op jit(solution)/shard_map/ppermute | solution.py:17
  23.3 1.0 fusion.1
  24.3 2.0 %collective-permute-start.2 = (bf16[512,128]{1,0:T(8,128)(2,1)S(1)}, bf16[512,128]{1,0:T(8,128)(2,1)S(1)}, u32[]{:S(2)}, u32[]{:S(2)}) collective-permute-start(bf16[512,128]{1,0:T(8,128)(2,1)S(1)} %bitcast.32), channel_id=1, source_target_pairs={{3,0},{0,1},{1,2},{2,3},{7,4},{4,5},{5,6},{6,7},{11,8},{8,9},{9,10... | collective-permute-start | bytes 393224 | tf_op jit(solution)/shard_map/ppermute | solution.py:17
  26.3 1.0 collective-permute-start.3
  27.3 0.8 fusion.5
  28.1 29.5 %edges.1.edge_ref = bf16[4096,128]{1,0:T(8,128)(2,1)} custom-call(s32[8,24,128]{2,1,0:T(8,128)} %bitcast.35, s32[8,24,128]{2,1,0:T(8,128)} %bitcast.33, s32[8,1,3072]{2,1,0:T(1,128)} %bitcast.34, bf16[4096,128]{1,0:T(8,128)(2,1)} %feat_ref.5, bf16[128,256]{1,0:T(8,128)(2,1)} %w_pair_ref.1, bf16[128,128]{1,0:T(8,128)(2,1)} %w_edge_ref.1), custom_call_target="tpu_custom_call" | custom-call | flops 9663676416 | bytes 2097152 | tf_op jit(solution)/shard_map/edges/pallas_call | solution.py:294
  59.1 27.4 %nodes.1 = (bf16[16384,128]{1,0:T(8,128)(2,1)}, bf16[4096,128]{1,0:T(8,128)(2,1)}, f32[3,4096]{1,0:T(4,128)}, bf16[8,144,128]{2,1,0:T(8,128)(2,1)}, f32[4,128]{1,0:T(4,128)}) custom-call(bf16[16384,128]{1,0:T(8,128)(2,1)} %encode.1.below_ref.centre_ref.above_ref, bf16[16384,128]{1,0:T(8,128)(2,1)} %encode.1.below_ref.centre_ref.above_ref, ...), custom_call_target="tpu_custom_call" | custom-call | tf_op jit(solution)/shard_map/nodes/pallas_call | solution.py:319
  86.5 5.0 %collective-permute-done.4 = f32[4,128]{1,0:T(4,128)S(1)} collective-permute-done((f32[4,128]{1,0:T(4,128)}, f32[4,128]{1,0:T(4,128)S(1)}, u32[]{:S(2)}, u32[]{:S(2)}) %collective-permute-start.4) | collective-permute-done | bytes 2080 | tf_op jit(solution)/shard_map/ppermute | solution.py:17
  92.2 5.4 %collective-permute-done.5 = f32[4,128]{1,0:T(4,128)S(1)} collective-permute-done((f32[4,128]{1,0:T(4,128)S(1)}, f32[4,128]{1,0:T(4,128)S(1)}, u32[]{:S(2)}, u32[]{:S(2)}) %collective-permute-start.5) | collective-permute-done | bytes 2080 | tf_op jit(solution)/shard_map/ppermute | solution.py:17
  97.6 4.5 %collective-permute-done.6 = f32[4,128]{1,0:T(4,128)S(1)} collective-permute-done((f32[4,128]{1,0:T(4,128)S(1)}, f32[4,128]{1,0:T(4,128)S(1)}, u32[]{:S(2)}, u32[]{:S(2)}) %collective-permute-start.6) | collective-permute-done | bytes 2080 | tf_op jit(solution)/shard_map/ppermute | solution.py:17
  102.1 1.0 collective-permute-start.7
  103.1 1.0 fusion.4
  104.1 2.5 %collective-permute-done.7 = f32[4,128]{1,0:T(4,128)S(1)} collective-permute-done((f32[4,128]{1,0:T(4,128)S(1)}, f32[4,128]{1,0:T(4,128)S(1)}, u32[]{:S(2)}, u32[]{:S(2)}) %collective-permute-start.7) | collective-permute-done | bytes 2080 | tf_op jit(solution)/shard_map/ppermute | solution.py:17
  106.6 1.9 %collective-permute-start.8 = (f32[4,128]{1,0:T(4,128)S(1)}, f32[4,128]{1,0:T(4,128)S(1)}, u32[]{:S(2)}, u32[]{:S(2)}) collective-permute-start(f32[4,128]{1,0:T(4,128)S(1)} %add.20), channel_id=1, source_target_pairs={{2,0},{3,1},{0,2},{1,3},{6,4},{7,5},{4,6},{5,7},{10,8},{11,9},{8,1... | collective-permute-start | bytes 6152 | tf_op jit(solution)/shard_map/ppermute | solution.py:17
  108.5 0.8 fusion.3
  109.3 3.5 %collective-permute-start.9 = (bf16[3,144,128]{2,1,0:T(8,128)(2,1)S(1)}, bf16[3,144,128]{2,1,0:T(8,128)(2,1)S(1)}, u32[]{:S(2)}, u32[]{:S(2)}) collective-permute-start(bf16[3,144,128]{2,1,0:T(8,128)(2,1)S(1)} %get-tuple-element.21), channel_id=1, source_target_pairs={{4,0},{8,4},{12,8},{16,12},{20,16},{24,20},{28,24},{0,28},{5,1},{9... | collective-permute-start | bytes 331784 | tf_op jit(solution)/shard_map/ppermute | solution.py:17
  113.6 1.7 %collective-permute-done.10 = bf16[3,144,128]{2,1,0:T(8,128)(2,1)S(1)} collective-permute-done((bf16[3,144,128]{2,1,0:T(8,128)(2,1)S(1)}, bf16[3,144,128]{2,1,0:T(8,128)(2,1)S(1)}, u32[]{:S(2)}, u32[]{:S(2)}) %collective-permute-start.10) | collective-permute-done | bytes 110624 | tf_op jit(solution)/shard_map/ppermute | solution.py:17
  116.1 4.1 %collective-permute-done.11 = bf16[3,144,128]{2,1,0:T(8,128)(2,1)S(1)} collective-permute-done((bf16[3,144,128]{2,1,0:T(8,128)(2,1)S(1)}, bf16[3,144,128]{2,1,0:T(8,128)(2,1)S(1)}, u32[]{:S(2)}, u32[]{:S(2)}) %collective-permute-start.11) | collective-permute-done | bytes 110624 | tf_op jit(solution)/shard_map/ppermute | solution.py:17
  120.2 1.6 %collective-permute-start.12 = (bf16[3,144,128]{2,1,0:T(8,128)(2,1)S(1)}, bf16[3,144,128]{2,1,0:T(8,128)(2,1)S(1)}, u32[]{:S(2)}, u32[]{:S(2)}) collective-permute-start(bf16[3,144,128]{2,1,0:T(8,128)(2,1)S(1)} %pad_maximum_fusion.1), channel_id=1, source_target_pairs={{3,0},{0,1},{1,2},{2,3},{7,4},{4,5},{5,6},{6,7},{11,8},{8,9},{9,10... | collective-permute-start | bytes 331784 | tf_op jit(solution)/shard_map/ppermute | solution.py:17
  121.8 1.5 %subtract_select_fusion = f32[3,4096]{1,0:T(4,128)} fusion(f32[3,4096]{1,0:T(4,128)} %get-tuple-element.12, f32[3]{0:T(128)S(1)} %slice_divide_fusion, pred[4096]{0:T(1024)(128)(4,1)S(1)} %broadcast_compare_fusion), kind=kLoop, calls=%fused_computation.2 | loop fusion | flops 24576 | bytes 102412 | tf_op jit(solution)/shard_map/jit(_where)/select_n | solution.py:383
  123.4 2.5 %collective-permute-done.12 = bf16[3,144,128]{2,1,0:T(8,128)(2,1)S(1)} collective-permute-done((bf16[3,144,128]{2,1,0:T(8,128)(2,1)S(1)}, bf16[3,144,128]{2,1,0:T(8,128)(2,1)S(1)}, u32[]{:S(2)}, u32[]{:S(2)}) %collective-permute-start.12) | collective-permute-done | bytes 110624 | tf_op jit(solution)/shard_map/ppermute | solution.py:17
  126.0 0.7 slice.137
  (53 shorter events, 5.0 us)
Async XLA Ops:
  0.6 26.7 %copy-start.2 = (s32[2,24576]{1,0:T(2,128)S(1)}, s32[2,24576]{1,0:T(2,128)}, u32[]{:S(2)}) copy-start(s32[2,24576]{1,0:T(2,128)} %param.16) | copy-start | bytes 589828
  18.7 39.5 %collective-permute-start = (bf16[1024,128]{1,0:T(8,128)(2,1)S(1)}, bf16[1024,128]{1,0:T(8,128)(2,1)S(1)}, u32[]{:S(2)}, u32[]{:S(2)}) collective-permute-start(bf16[1024,128]{1,0:T(8,128)(2,1)S(1)} %get-tuple-element.18), channel_id=1, source_target_pairs={{28,0},{0,4},{4,8},{8,12},{12,16},{16,20},{20,24},{24,28},{29,1},{... | collective-permute-start | bytes 786440 | tf_op jit(solution)/shard_map/ppermute | solution.py:17
  19.2 39.0 %collective-permute-start.1 = (bf16[1024,128]{1,0:T(8,128)(2,1)S(1)}, bf16[1024,128]{1,0:T(8,128)(2,1)S(1)}, u32[]{:S(2)}, u32[]{:S(2)}) collective-permute-start(bf16[1024,128]{1,0:T(8,128)(2,1)S(1)} %get-tuple-element.17), channel_id=1, source_target_pairs={{4,0},{8,4},{12,8},{16,12},{20,16},{24,20},{28,24},{0,28},{5,1},{9... | collective-permute-start | bytes 786440 | tf_op jit(solution)/shard_map/ppermute | solution.py:17
  24.3 33.9 %collective-permute-start.2 = (bf16[512,128]{1,0:T(8,128)(2,1)S(1)}, bf16[512,128]{1,0:T(8,128)(2,1)S(1)}, u32[]{:S(2)}, u32[]{:S(2)}) collective-permute-start(bf16[512,128]{1,0:T(8,128)(2,1)S(1)} %bitcast.32), channel_id=1, source_target_pairs={{3,0},{0,1},{1,2},{2,3},{7,4},{4,5},{5,6},{6,7},{11,8},{8,9},{9,10... | collective-permute-start | bytes 393224 | tf_op jit(solution)/shard_map/ppermute | solution.py:17
  26.3 31.9 %collective-permute-start.3 = (bf16[512,128]{1,0:T(8,128)(2,1)S(1)}, bf16[512,128]{1,0:T(8,128)(2,1)S(1)}, u32[]{:S(2)}, u32[]{:S(2)}) collective-permute-start(bf16[512,128]{1,0:T(8,128)(2,1)S(1)} %bitcast.31), channel_id=1, source_target_pairs={{1,0},{2,1},{3,2},{0,3},{5,4},{6,5},{7,6},{4,7},{9,8},{10,9},{11,1... | collective-permute-start | bytes 393224 | tf_op jit(solution)/shard_map/ppermute | solution.py:17
  28.1 29.5 %copy-start.6 = (bf16[3,128]{1,0:T(4,128)(2,1)S(1)}, bf16[3,128]{1,0:T(4,128)(2,1)}, u32[]{:S(2)}) copy-start(bf16[3,128]{1,0:T(4,128)(2,1)} %param.25) | copy-start | bytes 2308
  58.2 0.7 copy-start.4
  58.2 0.7 copy-start.5
  58.2 0.8 copy-start
  58.2 0.8 copy-start.1
  59.1 38.5 %copy-start.3 = (s32[4096]{0:T(1024)S(1)}, s32[4096]{0:T(1024)}, u32[]{:S(2)}) copy-start(s32[4096]{0:T(1024)} %param.17) | copy-start | bytes 49156
  86.5 5.1 %collective-permute-start.4 = (f32[4,128]{1,0:T(4,128)}, f32[4,128]{1,0:T(4,128)S(1)}, u32[]{:S(2)}, u32[]{:S(2)}) collective-permute-start(f32[4,128]{1,0:T(4,128)} %get-tuple-element.13), channel_id=1, source_target_pairs={{28,0},{0,4},{4,8},{8,12},{12,16},{16,20},{20,24},{24,28},{29,1},{... | collective-permute-start | bytes 6152 | tf_op jit(solution)/shard_map/ppermute | solution.py:17
  92.2 5.4 %collective-permute-start.5 = (f32[4,128]{1,0:T(4,128)S(1)}, f32[4,128]{1,0:T(4,128)S(1)}, u32[]{:S(2)}, u32[]{:S(2)}) collective-permute-start(f32[4,128]{1,0:T(4,128)S(1)} %add.17), channel_id=1, source_target_pairs={{24,0},{28,4},{0,8},{4,12},{8,16},{12,20},{16,24},{20,28},{25,1},{... | collective-permute-start | bytes 6152 | tf_op jit(solution)/shard_map/ppermute | solution.py:17
  97.6 4.5 %collective-permute-start.6 = (f32[4,128]{1,0:T(4,128)S(1)}, f32[4,128]{1,0:T(4,128)S(1)}, u32[]{:S(2)}, u32[]{:S(2)}) collective-permute-start(f32[4,128]{1,0:T(4,128)S(1)} %add.18), channel_id=1, source_target_pairs={{16,0},{20,4},{24,8},{28,12},{0,16},{4,20},{8,24},{12,28},{17,1},{... | collective-permute-start | bytes 6152 | tf_op jit(solution)/shard_map/ppermute | solution.py:17
  102.1 4.5 %collective-permute-start.7 = (f32[4,128]{1,0:T(4,128)S(1)}, f32[4,128]{1,0:T(4,128)S(1)}, u32[]{:S(2)}, u32[]{:S(2)}) collective-permute-start(f32[4,128]{1,0:T(4,128)S(1)} %add.19), channel_id=1, source_target_pairs={{3,0},{0,1},{1,2},{2,3},{7,4},{4,5},{5,6},{6,7},{11,8},{8,9},{9,10... | collective-permute-start | bytes 6152 | tf_op jit(solution)/shard_map/ppermute | solution.py:17
  106.6 6.3 %collective-permute-start.8 = (f32[4,128]{1,0:T(4,128)S(1)}, f32[4,128]{1,0:T(4,128)S(1)}, u32[]{:S(2)}, u32[]{:S(2)}) collective-permute-start(f32[4,128]{1,0:T(4,128)S(1)} %add.20), channel_id=1, source_target_pairs={{2,0},{3,1},{0,2},{1,3},{6,4},{7,5},{4,6},{5,7},{10,8},{11,9},{8,1... | collective-permute-start | bytes 6152 | tf_op jit(solution)/shard_map/ppermute | solution.py:17
  109.3 6.0 %collective-permute-start.10 = (bf16[3,144,128]{2,1,0:T(8,128)(2,1)S(1)}, bf16[3,144,128]{2,1,0:T(8,128)(2,1)S(1)}, u32[]{:S(2)}, u32[]{:S(2)}) collective-permute-start(bf16[3,144,128]{2,1,0:T(8,128)(2,1)S(1)} %get-tuple-element.22), channel_id=1, source_target_pairs={{28,0},{0,4},{4,8},{8,12},{12,16},{16,20},{20,24},{24,28},{29,1},{... | collective-permute-start | bytes 331784 | tf_op jit(solution)/shard_map/ppermute | solution.py:17
  109.3 6.0 %collective-permute-start.9 = (bf16[3,144,128]{2,1,0:T(8,128)(2,1)S(1)}, bf16[3,144,128]{2,1,0:T(8,128)(2,1)S(1)}, u32[]{:S(2)}, u32[]{:S(2)}) collective-permute-start(bf16[3,144,128]{2,1,0:T(8,128)(2,1)S(1)} %get-tuple-element.21), channel_id=1, source_target_pairs={{4,0},{8,4},{12,8},{16,12},{20,16},{24,20},{28,24},{0,28},{5,1},{9... | collective-permute-start | bytes 331784 | tf_op jit(solution)/shard_map/ppermute | solution.py:17
  115.3 4.8 %collective-permute-start.11 = (bf16[3,144,128]{2,1,0:T(8,128)(2,1)S(1)}, bf16[3,144,128]{2,1,0:T(8,128)(2,1)S(1)}, u32[]{:S(2)}, u32[]{:S(2)}) collective-permute-start(bf16[3,144,128]{2,1,0:T(8,128)(2,1)S(1)} %pad_maximum_fusion), channel_id=1, source_target_pairs={{1,0},{2,1},{3,2},{0,3},{5,4},{6,5},{7,6},{4,7},{9,8},{10,9},{11,1... | collective-permute-start | bytes 331784 | tf_op jit(solution)/shard_map/ppermute | solution.py:17
  120.2 5.7 %collective-permute-start.12 = (bf16[3,144,128]{2,1,0:T(8,128)(2,1)S(1)}, bf16[3,144,128]{2,1,0:T(8,128)(2,1)S(1)}, u32[]{:S(2)}, u32[]{:S(2)}) collective-permute-start(bf16[3,144,128]{2,1,0:T(8,128)(2,1)S(1)} %pad_maximum_fusion.1), channel_id=1, source_target_pairs={{3,0},{0,1},{1,2},{2,3},{7,4},{4,5},{5,6},{6,7},{11,8},{8,9},{9,10... | collective-permute-start | bytes 331784 | tf_op jit(solution)/shard_map/ppermute | solution.py:17
where the time goes:
time: 128 us; the launch traced here: 127 us
  Pallas kernels  73.8 us (58%)
  waiting for transfers between devices  25.7 us (20%)
  starting transfers between devices  15.9 us (12%)
  local copies, waits for them, and re-layouts  7.47 us (6%)
  other arithmetic  3.75 us (3%)
    pallas_call x1, Pallas kernels, shards(): pl.pallas_call(functools.partial(edge_kernel, members), grid=(count,), ou...  29.5 us
    pallas_call x1, Pallas kernels, shards(): pl.pallas_call(functools.partial(node_kernel, plane, cz, cap), grid=(coun...  27.4 us
    ppermute x13, waiting for transfers between devices, from_behind(): return lax.ppermute(block, axis, route)  25.7 us
    pallas_call x1, Pallas kernels, shards(): pl.pallas_call(functools.partial(encode_kernel, min(512, span)), grid=(co...  17 us
    ppermute x13, starting transfers between devices, from_behind(): return lax.ppermute(block, axis, route)  15.9 us
  transfers between devices with their start and end apart: 13, of which 7 were waited for; matrix products, arithmetic and copies ran while one was open for 6% of the time, Pallas kernels for 23%

commit v1 on v0

--- a/solution.py
+++ b/solution.py
@@ -9,23 +9,7 @@
 directions = ((-1, -1), (-1, 0), (-1, 1), (0, -1), (0, 1), (1, -1), (1, 0), (1, 1))
 LANES = 128
 VMEM_LIMIT = 60 * 1024 * 1024
-
-
-def from_behind(block, axis, distance):
-    devices = range(lax.axis_size(axis))
-    route = [((i - distance) % len(devices), i) for i in devices]
-    return lax.ppermute(block, axis, route)
-
-
-def summed_over(total, axis):
-    devices = lax.axis_size(axis)
-    if devices & (devices - 1):
-        return lax.psum(total, axis)
-    distance = 1
-    while distance < devices:
-        total = total + from_behind(total, axis, distance)
-        distance *= 2
-    return total
+MESH = pl.DeviceIdType.MESH
 
 
 def group_sizes(parts, cells):
@@ -43,9 +27,21 @@
     return jnp.dot(a, b, preferred_element_type=jnp.float32)
 
 
+def nt_dot(a, b):
+    return lax.dot_general(a, b, (((1,), (1,)), ((), ())), preferred_element_type=jnp.float32)
+
+
 def row_hot(keys, rows, first):
     lanes = lax.broadcasted_iota(jnp.int32, (rows, keys.shape[1]), 0) + first
     return jnp.where(lanes == keys, 1.0, 0.0).astype(jnp.bfloat16)
+
+
+def down_hot(keys, rows):
+    place = lax.broadcasted_iota(jnp.int32, (rows, keys.shape[1]), 0).astype(jnp.float32)
+    place = place.astype(jnp.bfloat16)
+    keys = keys.astype(jnp.float32).astype(jnp.bfloat16)
+    one = jnp.ones((), jnp.bfloat16)
+    return jnp.where(place == keys, one, jnp.zeros((), jnp.bfloat16))
 
 
 def col_hot(cols, start, stop, width):
@@ -57,49 +53,144 @@
     return jnp.concatenate(parts, axis=0)
 
 
-def encode_kernel(chunk, cell_ref, feat_ref, state_ref, w_enc_ref, out_ref):
-    span = state_ref.shape[0]
-    base = pl.program_id(0) * span
-    cells = cell_ref[0] - base
-
-    def body(i, carry):
-        first = pl.multiple_of(i * chunk, chunk)
-        onehot = row_hot(cells, chunk, first)
-        deposit = f32dot(onehot, feat_ref[...]).astype(jnp.bfloat16)
-        rows = pl.ds(first, chunk)
-        out_ref[rows, :] = (
-            state_ref[rows, :].astype(jnp.float32) + f32dot(deposit, w_enc_ref[...])
+def moved_by(axis, distance):
+    return lax.rem(lax.axis_index(axis) + distance + lax.axis_size(axis), lax.axis_size(axis))
+
+
+def greet(places):
+    barrier = pltpu.get_barrier_semaphore()
+    for dx, dy in places:
+        where = (moved_by("gx", dx), moved_by("gy", dy))
+        pl.semaphore_signal(barrier, inc=1, device_id=where, device_id_type=MESH)
+
+
+def front_kernel(
+    count,
+    plane,
+    depth,
+    chunk,
+    cell_ref,
+    cell_tile_ref,
+    feat_ref,
+    state_ref,
+    pairs_ref,
+    w_enc_ref,
+    w_pair_ref,
+    w_edge_ref,
+    mesh1_ref,
+    edge_ref,
+    xlo_ref,
+    xhi_ref,
+    ylo_ref,
+    yhi_ref,
+    xsend_ref,
+    ysend_ref,
+    send_sems,
+    recv_sems,
+):
+    turn = pl.program_id(0)
+    span, width = state_ref.shape
+    members = feat_ref.shape[0]
+    planes = span // plane
+    beside = ((1, 0), (-1, 0), (0, 1), (0, -1))
+
+    @pl.when(turn == 0)
+    def _():
+        greet(beside)
+
+    @pl.when(turn < count)
+    def _():
+        block = members // 2
+        half = span // 2
+        base = turn * span
+        cols = (cell_tile_ref[0] - base).T
+        grown = f32dot(feat_ref[...], w_enc_ref[...])
+        low, high = [], []
+        for j in range(members // LANES):
+            rows = grown[j * LANES : (j + 1) * LANES]
+            upper = cols[:, j : j + 1] >= half
+            low.append(jnp.where(upper, 0.0, rows))
+            high.append(jnp.where(upper, rows, 0.0))
+        both = jnp.concatenate(
+            [jnp.concatenate(low, axis=0), jnp.concatenate(high, axis=0)], axis=1
         ).astype(jnp.bfloat16)
-        return carry
-
-    lax.fori_loop(0, span // chunk, body, 0)
-
-
-def edge_kernel(
-    members, send_ref, recv_ref, recv_row_ref, feat_ref, w_pair_ref, w_edge_ref, out_ref
-):
-    base = pl.program_id(0) * members
-    width = feat_ref.shape[1]
-    proj = f32dot(feat_ref[...], w_pair_ref[...]).astype(jnp.bfloat16)
-    table = jnp.concatenate([proj[:, :width], proj[:, width:]], axis=0)
-    send_cols = (send_ref[0] - base).T
-    recv_cols = (recv_ref[0] - base).T
-    turns = send_cols.shape[1]
-    step = 6 if turns % 6 == 0 else 1
-    total = jnp.zeros((members, width), jnp.float32)
-    for start in range(0, turns, step):
-        hot = jnp.concatenate(
-            [
-                col_hot(send_cols, start, start + step, members),
-                col_hot(recv_cols, start, start + step, members),
-            ],
-            axis=1,
-        )
-        act = silu(f32dot(hot, table)).astype(jnp.bfloat16)
-        keys = recv_row_ref[0, :, start * LANES : (start + step) * LANES] - base
-        total = total + f32dot(row_hot(keys, members, 0), act)
-    edge_sum = f32dot(total.astype(jnp.bfloat16), w_edge_ref[...])
-    out_ref[...] = edge_sum.astype(jnp.bfloat16)
+        cells = cell_ref[...] - base
+        keys = jnp.where(cells >= half, cells - half, cells)
+        for q in range(half // block):
+            gain = f32dot(down_hot(keys - q * block, block), both)
+            for part in range(2):
+                rows = slice(part * half + q * block, part * half + (q + 1) * block)
+                mesh1_ref[rows, :] = (
+                    state_ref[rows, :].astype(jnp.float32)
+                    + gain[:, part * width : (part + 1) * width]
+                ).astype(jnp.bfloat16)
+        for p in range(planes):
+            first = p * plane
+            rows = pl.ds(pl.multiple_of((turn * planes + p) * depth, depth), depth)
+            ysend_ref[0, rows, :] = mesh1_ref[first + plane - depth : first + plane, :]
+            ysend_ref[1, rows, :] = mesh1_ref[first : first + depth, :]
+
+    @pl.when(turn == 0)
+    def _():
+        xsend_ref[1] = mesh1_ref[:plane, :]
+
+    @pl.when(turn == count - 1)
+    def _():
+        xsend_ref[0] = mesh1_ref[span - plane :, :]
+
+    def copies():
+        sources = (xsend_ref.at[0], xsend_ref.at[1], ysend_ref.at[0], ysend_ref.at[1])
+        targets = (xlo_ref, xhi_ref, ylo_ref, yhi_ref)
+        return [
+            pltpu.make_async_remote_copy(
+                src_ref=sources[k],
+                dst_ref=targets[k],
+                send_sem=send_sems.at[k],
+                recv_sem=recv_sems.at[k],
+                device_id=(moved_by("gx", dx), moved_by("gy", dy)),
+                device_id_type=MESH,
+            )
+            for k, (dx, dy) in enumerate(beside)
+        ]
+
+    @pl.when(turn == count)
+    def _():
+        pl.semaphore_wait(pltpu.get_barrier_semaphore(), len(beside))
+        for copy in copies():
+            copy.start()
+
+    @pl.when(turn >= count)
+    def _():
+        base = (turn - count) * members
+        half = members // 2
+        table = nt_dot(w_pair_ref[...].T, feat_ref[...]).astype(jnp.bfloat16)
+        tables = [
+            jnp.concatenate([table[:width, :half], table[:width, half:]], axis=0),
+            jnp.concatenate([table[width:, :half], table[width:, half:]], axis=0),
+        ]
+        zero = jnp.zeros((), jnp.bfloat16)
+        total = jnp.zeros((half, 2 * width), jnp.float32)
+        for first in range(0, pairs_ref.shape[1], chunk):
+            pre = None
+            for end in range(2):
+                rows = pairs_ref[end : end + 1, first : first + chunk] - base
+                upper = rows >= half
+                hot = down_hot(jnp.where(upper, rows - half, rows), half)
+                got = f32dot(tables[end], hot)
+                picked = jnp.where(upper, got[width:], got[:width])
+                pre = picked if pre is None else pre + picked
+            act = silu(pre)
+            acts = jnp.concatenate(
+                [jnp.where(upper, 0.0, act), jnp.where(upper, act, 0.0)], axis=0
+            ).astype(jnp.bfloat16)
+            total = total + nt_dot(hot, acts)
+        total = jnp.concatenate([total[:, :width], total[:, width:]], axis=0)
+        edge_ref[...] = f32dot(total.astype(jnp.bfloat16), w_edge_ref[...]).astype(jnp.bfloat16)
+
+    @pl.when(turn == 2 * count - 1)
+    def _():
+        for copy in copies():
+            copy.wait()
 
 
 def node_kernel(
@@ -218,11 +309,96 @@
             packed_ref[k, cap:, :] = moving[:16, rows].astype(jnp.bfloat16)
 
 
-def unpack(moving, drift):
-    values = moving.astype(jnp.float32)
-    weight = values[..., 3:4, :]
-    speed = jnp.where(weight > 0, values[..., :3, :] - drift[:, None], 0.0)
-    return jnp.concatenate([speed, weight], axis=-2)
+def meeting_places(nx, ny):
+    around = [(o, 0) for o in range(1, nx)] + [(0, o) for o in range(1, ny)]
+    around += [(dx % nx, dy % ny) for dx, dy in directions]
+    return [place for place in dict.fromkeys(around) if place != (0, 0)]
+
+
+def tail_kernel(
+    nx,
+    ny,
+    cap,
+    packed_ref,
+    totals_ref,
+    vel1_ref,
+    dest_ref,
+    feat_ref,
+    arrived_ref,
+    stay_ref,
+    xsum_ref,
+    part_ref,
+    ysum_ref,
+    got_ref,
+    send_x,
+    recv_x,
+    send_y,
+    recv_y,
+    send_f,
+    recv_f,
+    send_m,
+    recv_m,
+):
+    me_x, me_y = lax.axis_index("gx"), lax.axis_index("gy")
+    places = meeting_places(nx, ny)
+    greet(places)
+    xsum_ref[me_x] = totals_ref[...]
+    pl.semaphore_wait(pltpu.get_barrier_semaphore(), len(places))
+
+    def copy(source, target, sends, recvs, n, dx, dy):
+        made = pltpu.make_async_remote_copy(
+            src_ref=source,
+            dst_ref=target,
+            send_sem=sends.at[n],
+            recv_sem=recvs.at[n],
+            device_id=(moved_by("gx", dx), moved_by("gy", dy)),
+            device_id_type=MESH,
+        )
+        made.start()
+        return made
+
+    along_x = [
+        copy(totals_ref, xsum_ref.at[me_x], send_x, recv_x, o - 1, o, 0) for o in range(1, nx)
+    ]
+    moving = [
+        copy(packed_ref.at[k, pl.ds(cap, 16)], got_ref.at[k], send_m, recv_m, k, dx, dy)
+        for k, (dx, dy) in enumerate(directions)
+    ]
+    feats = [
+        copy(
+            packed_ref.at[k, pl.ds(0, cap)],
+            feat_ref.at[pl.ds(k * cap, cap)],
+            send_f,
+            recv_f,
+            k,
+            dx,
+            dy,
+        )
+        for k, (dx, dy) in enumerate(directions)
+    ]
+    for made in along_x:
+        made.wait()
+    part = jnp.sum(xsum_ref[...], axis=0)
+    part_ref[...] = part
+    ysum_ref[me_y] = part
+    along_y = [
+        copy(part_ref, ysum_ref.at[me_y], send_y, recv_y, o - 1, 0, o) for o in range(1, ny)
+    ]
+    for made in along_y:
+        made.wait()
+    sums = jnp.sum(jnp.sum(ysum_ref[...], axis=0), axis=1, keepdims=True)
+    drift = sums[:3] / sums[3:4]
+    stay_ref[...] = jnp.where(dest_ref[...] == 0, vel1_ref[...] - drift, 0.0)
+    for made in moving:
+        made.wait()
+    for k in range(len(directions)):
+        values = got_ref[k].astype(jnp.float32)
+        weight = values[3:4]
+        slots = slice(k * cap, (k + 1) * cap)
+        arrived_ref[:3, slots] = jnp.where(weight > 0, values[:3] - drift, 0.0)
+        arrived_ref[3:4, slots] = weight
+    for made in feats:
+        made.wait()
 
 
 def whole(shape):
@@ -253,6 +429,7 @@
     planes = span // plane
     per_group = pairs.shape[1] // count
     cap = parts // 32
+    nx, ny = lax.axis_size("gx"), lax.axis_size("gy")
     bf16, f32 = (jnp.bfloat16, jnp.float32)
     params = pltpu.CompilerParams(vmem_limit_bytes=VMEM_LIMIT)
 
@@ -261,57 +438,64 @@
     by_row = pl.BlockSpec((1, 1, members), lambda g: (g, 0, 0))
     by_tile = pl.BlockSpec((1, members // LANES, LANES), lambda g: (g, 0, 0))
 
-    cell_row = cell_index.reshape(count, 1, members)
     cell_tile = cell_index.reshape(count, members // LANES, LANES)
     dest_row = dest.reshape(count, 1, members)
     dest_tile = dest.reshape(count, members // LANES, LANES)
     mass_row = mass.reshape(count, 1, members)
-    send_tile = pairs[0].reshape(count, per_group // LANES, LANES)
-    recv_tile = pairs[1].reshape(count, per_group // LANES, LANES)
-    recv_row = pairs[1].reshape(count, 1, per_group)
     accel8 = jnp.pad(w_accel, ((0, 8 - w_accel.shape[0]), (0, 0)))
 
-    mesh1 = pl.pallas_call(
-        functools.partial(encode_kernel, min(512, span)),
-        grid=(count,),
-        out_shape=jax.ShapeDtypeStruct((cells, channels), bf16),
-        in_specs=[by_row, by_rows, by_cells, whole(w_enc.shape)],
-        out_specs=by_cells,
-        compiler_params=params,
-        cost_estimate=pl.CostEstimate(
-            flops=2 * cells * members * width, bytes_accessed=4 * cells * channels, transcendentals=0
-        ),
-        name="encode",
-    )(cell_row, part_feat, mesh_state.reshape(cells, channels), w_enc)
-
-    grid1 = mesh1.reshape(shape)
-    xlo = from_behind(grid1[cx - 1 :].reshape(plane, channels), "gx", 1)
-    xhi = from_behind(grid1[:1].reshape(plane, channels), "gx", -1)
-    ylo = from_behind(grid1[:, cy - 1 :].reshape(cx * cz, channels), "gy", 1)
-    yhi = from_behind(grid1[:, :1].reshape(cx * cz, channels), "gy", -1)
-
-    by_pairs = pl.BlockSpec((1, per_group // LANES, LANES), lambda g: (g, 0, 0))
-    edge_sum = pl.pallas_call(
-        functools.partial(edge_kernel, members),
-        grid=(count,),
-        out_shape=jax.ShapeDtypeStruct((parts, width), bf16),
+    early = lambda g: jnp.minimum(g, count - 1)
+    late = lambda g: jnp.maximum(g - count, 0)
+    anywhere = pl.BlockSpec(memory_space=pl.ANY)
+    mesh1, edge_sum, xlo, xhi, ylo, yhi = pl.pallas_call(
+        functools.partial(front_kernel, count, plane, cz, 512 if per_group % 512 == 0 else LANES),
+        grid=(2 * count,),
+        out_shape=(
+            jax.ShapeDtypeStruct((cells, channels), bf16),
+            jax.ShapeDtypeStruct((parts, width), bf16),
+            jax.ShapeDtypeStruct((plane, channels), bf16),
+            jax.ShapeDtypeStruct((plane, channels), bf16),
+            jax.ShapeDtypeStruct((cx * cz, channels), bf16),
+            jax.ShapeDtypeStruct((cx * cz, channels), bf16),
+        ),
         in_specs=[
-            by_pairs,
-            by_pairs,
-            pl.BlockSpec((1, 1, per_group), lambda g: (g, 0, 0)),
-            by_rows,
+            pl.BlockSpec((1, members), lambda g: (0, early(g))),
+            pl.BlockSpec((1, members // LANES, LANES), lambda g: (early(g), 0, 0)),
+            pl.BlockSpec((members, width), lambda g: (lax.rem(g, count), 0)),
+            pl.BlockSpec((span, channels), lambda g: (early(g), 0)),
+            pl.BlockSpec((2, per_group), lambda g: (0, late(g))),
+            whole(w_enc.shape),
             whole(w_pair.shape),
             whole(w_edge.shape),
         ],
-        out_specs=by_rows,
-        compiler_params=params,
-        cost_estimate=pl.CostEstimate(
-            flops=6 * pairs.shape[1] * members * width,
-            bytes_accessed=4 * parts * width,
-            transcendentals=pairs.shape[1] * width,
-        ),
-        name="edges",
-    )(send_tile, recv_tile, recv_row, part_feat, w_pair, w_edge)
+        out_specs=(
+            pl.BlockSpec((span, channels), lambda g: (early(g), 0)),
+            pl.BlockSpec((members, width), lambda g: (late(g), 0)),
+            anywhere,
+            anywhere,
+            anywhere,
+            anywhere,
+        ),
+        scratch_shapes=[
+            pltpu.VMEM((2, plane, channels), bf16),
+            pltpu.VMEM((2, cx * cz, channels), bf16),
+            pltpu.SemaphoreType.DMA((4,)),
+            pltpu.SemaphoreType.DMA((4,)),
+        ],
+        compiler_params=pltpu.CompilerParams(
+            vmem_limit_bytes=VMEM_LIMIT, collective_id=0, has_side_effects=True
+        ),
+        name="front",
+    )(
+        cell_index.reshape(1, parts),
+        cell_tile,
+        part_feat,
+        mesh_state.reshape(cells, channels),
+        pairs,
+        w_enc,
+        w_pair,
+        w_edge,
+    )
 
     one_plane = lambda f: pl.BlockSpec((plane, channels), f)
     by_layer = pl.BlockSpec((planes * cz, channels), lambda g: (g, 0))
@@ -378,20 +562,36 @@
         accel8,
     )
 
-    sums = jnp.sum(summed_over(summed_over(totals, "gx"), "gy"), axis=1)
-    drift = sums[:3] / sums[3]
-    stay_vel = jnp.where((dest == 0)[None, :], vel1 - drift[:, None], 0.0)
-
-    got = [packed[k] for k in range(8)]
-    for axis, part in (("gx", 0), ("gy", 1)):
-        for distance in (1, -1):
-            chosen = [k for k, offset in enumerate(directions) if offset[part] == distance]
-            moved = from_behind(jnp.stack([got[k] for k in chosen], axis=0), axis, distance)
-            for place, k in enumerate(chosen):
-                got[k] = moved[place]
-    arrived = jnp.stack(got, axis=0)
-    arrived_feat = arrived[:, :cap].reshape(-1, width)
-    arrived_vel = unpack(arrived[:, cap : cap + 4], drift).transpose(1, 0, 2).reshape(4, -1)
+    inside = pl.BlockSpec(memory_space=pltpu.VMEM)
+    dma = lambda n: pltpu.SemaphoreType.DMA((n,))
+    arrived_feat, arrived_vel, stay_vel = pl.pallas_call(
+        functools.partial(tail_kernel, nx, ny, cap),
+        out_shape=(
+            jax.ShapeDtypeStruct((8 * cap, width), bf16),
+            jax.ShapeDtypeStruct((4, 8 * cap), f32),
+            jax.ShapeDtypeStruct((3, parts), f32),
+        ),
+        in_specs=[inside] * 4,
+        out_specs=(anywhere, inside, inside),
+        scratch_shapes=[
+            pltpu.VMEM((nx, 4, LANES), f32),
+            pltpu.VMEM((4, LANES), f32),
+            pltpu.VMEM((ny, 4, LANES), f32),
+            pltpu.VMEM((8, 16, LANES), bf16),
+            dma(nx - 1),
+            dma(nx - 1),
+            dma(ny - 1),
+            dma(ny - 1),
+            dma(8),
+            dma(8),
+            dma(8),
+            dma(8),
+        ],
+        compiler_params=pltpu.CompilerParams(
+            vmem_limit_bytes=16 * 1024 * 1024, collective_id=1, has_side_effects=True
+        ),
+        name="tail",
+    )(packed, totals, vel1, dest.reshape(1, parts))
     return (mesh2.reshape(shape), stay_feat, stay_vel, arrived_feat, arrived_vel)
 
 

time: 128 us -> 79.4 us (0.62)
  waiting for transfers between devices: 25.7 us -> 0 us
  starting transfers between devices: 15.9 us -> 0 us
  other arithmetic: 3.75 us -> 0 us
  local copies, waits for them, and re-layouts: 7.47 us -> 5.68 us
    ppermute x13 -> x0, waiting for transfers between devices: 25.7 us -> none  [from_behind(): return lax.ppermute(block, axis, route)]
    ppermute x13 -> x0, starting transfers between devices: 15.9 us -> none  [from_behind(): return lax.ppermute(block, axis, route)]
    slice x11 -> x0, local copies, waits for them, and re-layouts: 5.97 us -> none  [the longest x2 1.76 us: shards(): got = [packed[k] for k in range(8)]]
    unnamed x21 -> x11, local copies, waits for them, and re-layouts: 0.9 us -> 4.42 us
    select_n x2 -> x0, other arithmetic: 1.62 us -> none  [the longest x1 1.55 us: shards(): stay_vel = jnp.where((dest == 0)[None, :], vel1 - drift[:, None], 0.0)]
    pallas_call x2, Pallas kernels: 46.4 us -> 45.1 us  [the longest x1 31.2 us: shards(): pl.pallas_call(functools.partial(front_kernel, count, plane, cz, 512 if p...]
  transfers between devices with their start and end apart: 13 -> 0, of which waited for: 7 -> 0; matrix products, arithmetic and copies ran while one was open for 6% -> 0% of each run, Pallas kernels for 23% -> 0%
where the time goes in v1:
time: 79.4 us; the launch traced here: 78.9 us
  Pallas kernels  72.6 us (91%)
  local copies, waits for them, and re-layouts  5.68 us (7%)
    pallas_call x1, Pallas kernels, shards(): pl.pallas_call(functools.partial(front_kernel, count, plane, cz, 512 if p...  31.2 us
    pallas_call x1, Pallas kernels, shards(): pl.pallas_call(functools.partial(node_kernel, plane, cz, cap), grid=(coun...  27.4 us
    pallas_call x1, Pallas kernels, shards(): pl.pallas_call(functools.partial(tail_kernel, nx, ny, cap), out_shape=(ja...  13.9 us
    unnamed x11, local copies, waits for them, and re-layouts  4.42 us

profile of v1, /device:TPU:0, one launch (start us, length us, event | category | flops | bytes accessed | tf_op | source)
XLA Modules:
  0.0 78.9 jit_solution(15992957402386334142)
XLA Ops:
  0.6 1.3 %pad.4.w_accel_ref = bf16[8,128]{1,0:T(8,128)(2,1)} pad(bf16[3,128]{1,0:T(4,128)(2,1)} %param.25, bf16[]{:T(256)} %constant.2.clone.1), padding=0_5x0_0 | pad | bytes 2818 | tf_op jit(solution)/shard_map/jit(_pad)/pad | solution.py:445
  1.9 31.2 %front.1 = (bf16[16384,128]{1,0:T(8,128)(2,1)}, bf16[4096,128]{1,0:T(8,128)(2,1)}, bf16[1024,128]{1,0:T(8,128)(2,1)}, bf16[1024,128]{1,0:T(8,128)(2,1)}, bf16[51...) custom-call(s32[1,4096]{1,0:T(1,128)} %bitcast.12, s32[8,4,128]{2,1,0:T(4,128)} %bitcast.13, bf16[4096,128]{1,0:T(8,128)(2,1)} %feat_ref.3, ...), custom_call_target="tpu_custom_call" | custom-call | tf_op jit(solution)/shard_map/front/pallas_call | solution.py:450
  33.1 0.0 copy-start.1
  33.1 27.4 %nodes.1 = (bf16[16384,128]{1,0:T(8,128)(2,1)}, bf16[4096,128]{1,0:T(8,128)(2,1)}, f32[3,4096]{1,0:T(4,128)}, bf16[8,144,128]{2,1,0:T(8,128)(2,1)}, f32[4,128]{1,0:T(4,128)}) custom-call(bf16[16384,128]{1,0:T(8,128)(2,1)} %get-tuple-element.19.below_ref.centre_ref.above_ref, bf16[16384,128]{1,0:T(8,128)(2,1)} %get-tuple-element.19.below_ref.centre_ref.above_ref, ...), custom_call_target="tpu_custom_call" | custom-call | tf_op jit(solution)/shard_map/nodes/pallas_call | solution.py:503
  60.6 0.0 copy-done.1
  60.6 0.0 copy-start
  60.6 1.0 %copy-done = bf16[8,144,128]{2,1,0:T(8,128)(2,1)S(1)} copy-done((bf16[8,144,128]{2,1,0:T(8,128)(2,1)S(1)}, bf16[8,144,128]{2,1,0:T(8,128)(2,1)}, u32[]{:S(2)}) %copy-start) | copy-done | bytes 294936
  61.5 0.0 copy-start.2
  61.5 0.8 %copy-done.2 = f32[3,4096]{1,0:T(4,128)S(1)} copy-done((f32[3,4096]{1,0:T(4,128)S(1)}, f32[3,4096]{1,0:T(4,128)}, u32[]{:S(2)}) %copy-start.2) | copy-done | bytes 49176
  62.4 0.0 copy-start.3
  62.4 0.7 copy-done.3
  63.0 13.9 %tail.1 = (bf16[1024,128]{1,0:T(8,128)(2,1)S(1)}, f32[4,1024]{1,0:T(4,128)S(1)}, f32[3,4096]{1,0:T(4,128)S(1)}) custom-call(bf16[8,144,128]{2,1,0:T(8,128)(2,1)S(1)} %copy-done, f32[4,128]{1,0:T(4,128)S(1)} %copy-done.3, f32[3,4096]{1,0:T(4,128)S(1)} %copy-done.2, s32[1,4096]{1,0:T(1,128)S(1)} %bitcast.10), custom_call_target="tpu_custom_call" | custom-call | tf_op jit(solution)/shard_map/tail/pallas_call | solution.py:567
  77.0 0.6 copy.21
  77.6 0.7 copy.22
  78.3 0.6 copy.23
Async XLA Ops:
  33.1 27.4 %copy-start.1 = (s32[4096]{0:T(1024)S(1)}, s32[4096]{0:T(1024)}, u32[]{:S(2)}) copy-start(s32[4096]{0:T(1024)} %param.17) | copy-start | bytes 49156
  60.6 1.0 %copy-start = (bf16[8,144,128]{2,1,0:T(8,128)(2,1)S(1)}, bf16[8,144,128]{2,1,0:T(8,128)(2,1)}, u32[]{:S(2)}) copy-start(bf16[8,144,128]{2,1,0:T(8,128)(2,1)} %get-tuple-element.27.packed_ref) | copy-start | bytes 884740
  61.5 0.8 %copy-start.2 = (f32[3,4096]{1,0:T(4,128)S(1)}, f32[3,4096]{1,0:T(4,128)}, u32[]{:S(2)}) copy-start(f32[3,4096]{1,0:T(4,128)} %get-tuple-element.29.vel1_ref) | copy-start | bytes 147460
  62.4 0.7 copy-start.3

commit v2 on v1

v2 whole, which is shorter than its diff:
```python
import functools
import jax
import jax.numpy as jnp
from jax import lax
from jax.experimental import pallas as pl
from jax.experimental.pallas import tpu as pltpu
from jax.sharding import PartitionSpec as P

directions = ((-1, -1), (-1, 0), (-1, 1), (0, -1), (0, 1), (1, -1), (1, 0), (1, 1))
LANES = 128
VMEM_LIMIT = 60 * 1024 * 1024
CHUNK = 512
MESH = pl.DeviceIdType.MESH


def group_sizes(parts, cells):
    members = min(512, parts)
    count = parts // members
    return (members, count, cells // count)


def silu_of_twice(half):
    return half + half * jnp.tanh(half)


def f32dot(a, b):
    return jnp.dot(a, b, preferred_element_type=jnp.float32)


def nt_dot(a, b):
    return lax.dot_general(a, b, (((1,), (1,)), ((), ())), preferred_element_type=jnp.float32)


def down_hot(keys, rows):
    place = lax.broadcasted_iota(jnp.int32, (rows, keys.shape[1]), 0).astype(jnp.float32)
    place = place.astype(jnp.bfloat16)
    keys = keys.astype(jnp.float32).astype(jnp.bfloat16)
    one = jnp.ones((), jnp.bfloat16)
    return jnp.where(place == keys, one, jnp.zeros((), jnp.bfloat16))


def over_hot(keys, width):
    place = lax.broadcasted_iota(jnp.int32, (keys.shape[0], width), 1).astype(jnp.int16)
    keys = jnp.broadcast_to(keys, (keys.shape[0], LANES)).astype(jnp.int16)
    keys = jnp.concatenate([keys] * (width // LANES), axis=1)
    return jnp.where(place == keys, jnp.ones((), jnp.bfloat16), jnp.zeros((), jnp.bfloat16))


def moved_by(axis, distance):
    return lax.rem(lax.axis_index(axis) + distance + lax.axis_size(axis), lax.axis_size(axis))


def greet(places):
    barrier = pltpu.get_barrier_semaphore()
    for dx, dy in places:
        where = (moved_by("gx", dx), moved_by("gy", dy))
        pl.semaphore_signal(barrier, inc=1, device_id=where, device_id_type=MESH)


def front_kernel(
    turns,
    plane,
    depth,
    chunk,
    cell_ref,
    cell_tile_ref,
    enc_feat_ref,
    state_ref,
    feat_ref,
    pairs_ref,
    w_enc_ref,
    w_pair_ref,
    w_edge_ref,
    mesh1_ref,
    edge_ref,
    xlo_ref,
    xhi_ref,
    ylo_ref,
    yhi_ref,
    xsend_ref,
    ysend_ref,
    half_pair_ref,
    send_sems,
    recv_sems,
):
    turn = pl.program_id(0)
    last = pl.num_programs(0) - 1
    members, width = feat_ref.shape
    groups = cell_tile_ref.shape[0]
    span = state_ref.shape[0] // groups
    planes = state_ref.shape[0] // plane
    beside = ((1, 0), (-1, 0), (0, 1), (0, -1))
    half = members // 2

    def copies():
        sources = (xsend_ref.at[0], xsend_ref.at[1], ysend_ref.at[0], ysend_ref.at[1])
        targets = (xlo_ref, xhi_ref, ylo_ref, yhi_ref)
        return [
            pltpu.make_async_remote_copy(
                src_ref=sources[k],
                dst_ref=targets[k],
                send_sem=send_sems.at[k],
                recv_sem=recv_sems.at[k],
                device_id=(moved_by("gx", dx), moved_by("gy", dy)),
                device_id_type=MESH,
            )
            for k, (dx, dy) in enumerate(beside)
        ]

    @pl.when(turn == 0)
    def _():
        greet(beside)
        half_pair_ref[...] = (0.5 * w_pair_ref[...].astype(jnp.float32)).T.astype(jnp.bfloat16)

    @pl.when(turn == turns)
    def _():
        pl.semaphore_wait(pltpu.get_barrier_semaphore(), len(beside))
        for copy in copies():
            copy.start()

    @pl.when(turn < turns)
    def _():
        top = span // 2
        for g in range(groups):
            base = (turn * groups + g) * span
            mine = slice(g * members, (g + 1) * members)
            cols = (cell_tile_ref[g] - base).T
            grown = f32dot(enc_feat_ref[mine, :], w_enc_ref[...])
            low, high = [], []
            for j in range(members // LANES):
                rows = grown[j * LANES : (j + 1) * LANES]
                upper = cols[:, j : j + 1] >= top
                low.append(jnp.where(upper, 0.0, rows))
                high.append(jnp.where(upper, rows, 0.0))
            both = jnp.concatenate(
                [jnp.concatenate(low, axis=0), jnp.concatenate(high, axis=0)], axis=1
            ).astype(jnp.bfloat16)
            cells = cell_ref[:, mine] - base
            keys = jnp.where(cells >= top, cells - top, cells)
            for q in range(top // half):
                gain = f32dot(down_hot(keys - q * half, half), both)
                for part in range(2):
                    first = g * span + part * top + q * half
                    rows = slice(first, first + half)
                    mesh1_ref[rows, :] = (
                        state_ref[rows, :].astype(jnp.float32)
                        + gain[:, part * width : (part + 1) * width]
                    ).astype(jnp.bfloat16)
        for p in range(planes):
            first = p * plane
            rows = pl.ds(pl.multiple_of((turn * planes + p) * depth, depth), depth)
            ysend_ref[0, rows, :] = mesh1_ref[first + plane - depth : first + plane, :]
            ysend_ref[1, rows, :] = mesh1_ref[first : first + depth, :]

    @pl.when(turn == 0)
    def _():
        xsend_ref[1] = mesh1_ref[:plane, :]

    @pl.when(turn == turns - 1)
    def _():
        xsend_ref[0] = mesh1_ref[(planes - 1) * plane :, :]

    base = turn * members
    table = nt_dot(half_pair_ref[...], feat_ref[...]).astype(jnp.bfloat16)
    tables = [
        jnp.concatenate([table[:width, :half], table[:width, half:]], axis=0),
        jnp.concatenate([table[width:, :half], table[width:, half:]], axis=0),
    ]
    total = jnp.zeros((half, 2 * width), jnp.float32)
    for first in range(0, pairs_ref.shape[1], chunk):
        pre = None
        for end in range(2):
            rows = pairs_ref[end : end + 1, first : first + chunk] - base
            upper = rows >= half
            hot = down_hot(jnp.where(upper, rows - half, rows), half)
            got = f32dot(tables[end], hot)
            picked = jnp.where(upper, got[width:], got[:width])
            pre = picked if pre is None else pre + picked
        act = silu_of_twice(pre).astype(jnp.bfloat16)
        share = jnp.where(upper, 1.0, 0.0)
        acts = jnp.concatenate(
            [act * (1.0 - share).astype(jnp.bfloat16), act * share.astype(jnp.bfloat16)], axis=0
        )
        total = total + nt_dot(hot, acts)
    total = jnp.concatenate([total[:, :width], total[:, width:]], axis=0)
    edge_ref[...] = f32dot(total.astype(jnp.bfloat16), w_edge_ref[...]).astype(jnp.bfloat16)

    @pl.when(turn == last)
    def _():
        for copy in copies():
            copy.wait()


def node_kernel(
    plane,
    depth,
    cap,
    below_ref,
    centre_ref,
    above_ref,
    xlo_ref,
    xhi_ref,
    ylo_ref,
    yhi_ref,
    cell_ref,
    dest_ref,
    dest_row_ref,
    edge_ref,
    feat_ref,
    mass_ref,
    vel_ref,
    w_mesh_ref,
    w_node_ref,
    w_accel_ref,
    mesh_ref,
    stay_ref,
    vel1_ref,
    packed_ref,
    total_ref,
    slots_ref,
    carry_ref,
    near_w_ref,
    wide_w_ref,
    node_w_ref,
    before_ref,
):
    step = pl.program_id(0)
    last = pl.num_programs(0) - 1
    span, width = centre_ref.shape
    members = feat_ref.shape[0]
    planes = span // plane
    base = step * span
    block = 2 * LANES

    @pl.when(step == 0)
    def _():
        slots_ref[...] = jnp.zeros_like(slots_ref)
        carry_ref[...] = jnp.zeros_like(carry_ref)
        total_ref[...] = jnp.zeros_like(total_ref)
        row = lax.broadcasted_iota(jnp.int32, (block, block), 0)
        col = lax.broadcasted_iota(jnp.int32, (block, block), 1)
        gap = row - col
        up_down = (jnp.abs(gap) == 1) & (row // depth == col // depth)
        near_w_ref[...] = jnp.where(up_down | (jnp.abs(gap) == depth), 1.0, 0.0).astype(
            jnp.bfloat16
        )
        scaled = 0.5 * w_mesh_ref[...].astype(jnp.float32)
        none = jnp.zeros_like(scaled)
        wide_w_ref[...] = jnp.concatenate(
            [
                jnp.concatenate([scaled, none], axis=1),
                jnp.concatenate([none, scaled], axis=1),
            ],
            axis=0,
        ).astype(jnp.bfloat16)
        node_w_ref[...] = (0.5 * w_node_ref[...].astype(jnp.float32)).astype(jnp.bfloat16)
        before_ref[...] = jnp.where(
            lax.broadcasted_iota(jnp.int32, (LANES, LANES), 0)
            < lax.broadcasted_iota(jnp.int32, (LANES, LANES), 1),
            1.0,
            0.0,
        ).astype(jnp.bfloat16)

    def wide(rows):
        return rows.astype(jnp.float32)

    for p in range(planes):
        for pair in range(0, plane, 2 * block):
            firsts = [p * plane + pair, p * plane + pair + block]
            raw = [centre_ref[f : f + block, :] for f in firsts]
            around = f32dot(near_w_ref[...], jnp.concatenate(raw, axis=1))
            sides = []
            for n, f in enumerate(firsts):
                rows = slice(f, f + block)
                inner = slice(f - p * plane, f - p * plane + block)
                if p == 0:
                    below = jnp.where(step == 0, xlo_ref[inner, :], below_ref[inner, :])
                else:
                    below = centre_ref[f - plane : f - plane + block, :]
                if p == planes - 1:
                    above = jnp.where(step == last, xhi_ref[inner, :], above_ref[inner, :])
                else:
                    above = centre_ref[f + plane : f + plane + block, :]
                if inner.start == 0:
                    left = ylo_ref[p * depth : (p + 1) * depth, :]
                else:
                    left = centre_ref[f - depth : f, :]
                if inner.stop == plane:
                    right = yhi_ref[p * depth : (p + 1) * depth, :]
                else:
                    right = centre_ref[f + block : f + block + depth, :]
                total = around[:, n * width : (n + 1) * width] + (wide(below) + wide(above))
                sides.append(
                    jnp.concatenate(
                        [
                            total[:depth] + wide(left),
                            total[depth:-depth],
                            total[-depth:] + wide(right),
                        ],
                        axis=0,
                    ).astype(jnp.bfloat16)
                )
            gain = silu_of_twice(f32dot(jnp.concatenate(sides, axis=1), wide_w_ref[...]))
            for n, f in enumerate(firsts):
                mesh_ref[f : f + block, :] = (
                    wide(raw[n]) + gain[:, n * width : (n + 1) * width]
                ).astype(jnp.bfloat16)

    turns = members // LANES
    top = span // 2
    cell_cols = (cell_ref[0] - base).T
    dest_cols = dest_ref[0].T
    hots, uppers = [], []
    for j in range(turns):
        col = cell_cols[:, j : j + 1]
        upper = col >= top
        uppers.append(upper)
        hots.append(over_hot(jnp.where(upper, col - top, col), top))
    pair = jnp.concatenate([mesh_ref[:top, :], mesh_ref[top:, :]], axis=1)
    found = f32dot(jnp.concatenate(hots, axis=0), pair)
    near = jnp.concatenate(
        [
            jnp.where(
                uppers[j],
                found[j * LANES : (j + 1) * LANES, width:],
                found[j * LANES : (j + 1) * LANES, :width],
            )
            for j in range(turns)
        ],
        axis=0,
    ).astype(jnp.bfloat16)
    update = f32dot(jnp.concatenate([edge_ref[...], near], axis=1), node_w_ref[...])
    h_new = (wide(feat_ref[...]) + silu_of_twice(update)).astype(jnp.bfloat16)
    h_wide = h_new.astype(jnp.float32)
    for j in range(turns):
        rows = slice(j * LANES, (j + 1) * LANES)
        stay_ref[rows, :] = jnp.where(dest_cols[:, j : j + 1] == 0, h_wide[rows], 0.0).astype(
            jnp.bfloat16
        )
    vel1 = vel_ref[...] + nt_dot(w_accel_ref[...], h_new)
    mass = mass_ref[...]
    vel1_ref[...] = vel1
    sums = jnp.concatenate([mass * vel1, mass], axis=0)
    total_ref[...] += sum(sums[:, j * LANES : (j + 1) * LANES] for j in range(turns))

    dest = dest_row_ref[...]
    ways = lax.broadcasted_iota(jnp.int32, (8, members), 0) + 1
    chosen = jnp.where(ways == dest, 1.0, 0.0)
    stacked = jnp.concatenate([chosen[:, j * LANES : (j + 1) * LANES] for j in range(turns)], axis=0)
    earlier = f32dot(stacked.astype(jnp.bfloat16), before_ref[...])
    counts = jnp.sum(stacked, axis=1, keepdims=True)
    done = carry_ref[:, :1]
    places = []
    for j in range(turns):
        rows = slice(8 * j, 8 * (j + 1))
        places.append(jnp.where(stacked[rows] > 0, earlier[rows] + done, -1.0))
        done = done + counts[rows]
    carry_ref[...] = jnp.broadcast_to(done, carry_ref.shape)
    place = jnp.concatenate(places, axis=1)
    extra = jnp.concatenate([vel1, mass, jnp.zeros((LANES - 4, members), jnp.float32)], axis=0)
    values = jnp.concatenate([h_new, extra.T.astype(jnp.bfloat16)], axis=1)
    for k in range(8):
        rows = slice(k * cap, (k + 1) * cap)
        slots_ref[rows, :] += f32dot(down_hot(place[k : k + 1], cap), values).astype(jnp.bfloat16)

    @pl.when(step == last)
    def _():
        moving = wide(slots_ref[:, width:]).T
        for k in range(8):
            rows = slice(k * cap, (k + 1) * cap)
            packed_ref[k, :cap, :] = slots_ref[rows, :width]
            packed_ref[k, cap:, :] = moving[:16, rows].astype(jnp.bfloat16)


def meeting_places(nx, ny):
    around = [(o, 0) for o in range(1, nx)] + [(0, o) for o in range(1, ny)]
    around += [(dx % nx, dy % ny) for dx, dy in directions]
    return [place for place in dict.fromkeys(around) if place != (0, 0)]


def tail_kernel(
    nx,
    ny,
    cap,
    packed_ref,
    totals_ref,
    vel1_ref,
    dest_ref,
    feat_ref,
    arrived_ref,
    stay_ref,
    xsum_ref,
    part_ref,
    ysum_ref,
    got_ref,
    send_x,
    recv_x,
    send_y,
    recv_y,
    send_f,
    recv_f,
    send_m,
    recv_m,
):
    me_x, me_y = lax.axis_index("gx"), lax.axis_index("gy")
    places = meeting_places(nx, ny)
    greet(places)
    xsum_ref[me_x] = totals_ref[...]
    pl.semaphore_wait(pltpu.get_barrier_semaphore(), len(places))

    def copy(source, target, sends, recvs, n, dx, dy):
        made = pltpu.make_async_remote_copy(
            src_ref=source,
            dst_ref=target,
            send_sem=sends.at[n],
            recv_sem=recvs.at[n],
            device_id=(moved_by("gx", dx), moved_by("gy", dy)),
            device_id_type=MESH,
        )
        made.start()
        return made

    along_x = [
        copy(totals_ref, xsum_ref.at[me_x], send_x, recv_x, o - 1, o, 0) for o in range(1, nx)
    ]
    moving = [
        copy(packed_ref.at[k, pl.ds(cap, 16)], got_ref.at[k], send_m, recv_m, k, dx, dy)
        for k, (dx, dy) in enumerate(directions)
    ]
    feats = [
        copy(
            packed_ref.at[k, pl.ds(0, cap)],
            feat_ref.at[pl.ds(k * cap, cap)],
            send_f,
            recv_f,
            k,
            dx,
            dy,
        )
        for k, (dx, dy) in enumerate(directions)
    ]
    for made in along_x:
        made.wait()
    part = jnp.sum(xsum_ref[...], axis=0)
    part_ref[...] = part
    ysum_ref[me_y] = part
    along_y = [
        copy(part_ref, ysum_ref.at[me_y], send_y, recv_y, o - 1, 0, o) for o in range(1, ny)
    ]
    for made in along_y:
        made.wait()
    sums = jnp.sum(jnp.sum(ysum_ref[...], axis=0), axis=1, keepdims=True)
    drift = sums[:3] / sums[3:4]
    stay_ref[...] = jnp.where(dest_ref[...] == 0, vel1_ref[...] - drift, 0.0)
    for made in moving:
        made.wait()
    for k in range(len(directions)):
        values = got_ref[k].astype(jnp.float32)
        weight = values[3:4]
        slots = slice(k * cap, (k + 1) * cap)
        arrived_ref[:3, slots] = jnp.where(weight > 0, values[:3] - drift, 0.0)
        arrived_ref[3:4, slots] = weight
    for made in feats:
        made.wait()


def whole(shape):
    return pl.BlockSpec(shape, lambda g: (0,) * len(shape))


def shards(
    mesh_state,
    part_feat,
    cell_index,
    pairs,
    dest,
    mass,
    velocity,
    w_enc,
    w_mesh,
    w_pair,
    w_edge,
    w_node,
    w_accel,
):
    shape = mesh_state.shape
    parts, width = part_feat.shape
    cx, cy, cz, channels = shape
    cells = cx * cy * cz
    plane = cy * cz
    members, count, span = group_sizes(parts, cells)
    planes = span // plane
    per_group = pairs.shape[1] // count
    cap = parts // 32
    nx, ny = lax.axis_size("gx"), lax.axis_size("gy")
    bf16, f32 = (jnp.bfloat16, jnp.float32)
    params = pltpu.CompilerParams(vmem_limit_bytes=VMEM_LIMIT)

    by_rows = pl.BlockSpec((members, width), lambda g: (g, 0))
    by_cells = pl.BlockSpec((span, channels), lambda g: (g, 0))
    by_row = pl.BlockSpec((1, members), lambda g: (0, g))
    by_tile = pl.BlockSpec((1, members // LANES, LANES), lambda g: (g, 0, 0))

    cell_tile = cell_index.reshape(count, members // LANES, LANES)
    dest_row = dest.reshape(1, parts)
    dest_tile = dest.reshape(count, members // LANES, LANES)
    mass_row = mass.reshape(1, parts)

    groups = 2
    turns = count // groups
    early = lambda g: jnp.minimum(g, turns - 1)
    anywhere = pl.BlockSpec(memory_space=pl.ANY)
    mesh1, edge_sum, xlo, xhi, ylo, yhi = pl.pallas_call(
        functools.partial(front_kernel, turns, plane, cz, CHUNK),
        grid=(count,),
        out_shape=(
            jax.ShapeDtypeStruct((cells, channels), bf16),
            jax.ShapeDtypeStruct((parts, width), bf16),
            jax.ShapeDtypeStruct((plane, channels), bf16),
            jax.ShapeDtypeStruct((plane, channels), bf16),
            jax.ShapeDtypeStruct((cx * cz, channels), bf16),
            jax.ShapeDtypeStruct((cx * cz, channels), bf16),
        ),
        in_specs=[
            pl.BlockSpec((1, groups * members), lambda g: (0, early(g))),
            pl.BlockSpec((groups, members // LANES, LANES), lambda g: (early(g), 0, 0)),
            pl.BlockSpec((groups * members, width), lambda g: (early(g), 0)),
            pl.BlockSpec((groups * span, channels), lambda g: (early(g), 0)),
            by_rows,
            pl.BlockSpec((2, per_group), lambda g: (0, g)),
            whole(w_enc.shape),
            whole(w_pair.shape),
            whole(w_edge.shape),
        ],
        out_specs=(
            pl.BlockSpec((groups * span, channels), lambda g: (early(g), 0)),
            by_rows,
            anywhere,
            anywhere,
            anywhere,
            anywhere,
        ),
        scratch_shapes=[
            pltpu.VMEM((2, plane, channels), bf16),
            pltpu.VMEM((2, cx * cz, channels), bf16),
            pltpu.VMEM((2 * width, width), bf16),
            pltpu.SemaphoreType.DMA((4,)),
            pltpu.SemaphoreType.DMA((4,)),
        ],
        compiler_params=pltpu.CompilerParams(
            vmem_limit_bytes=VMEM_LIMIT, collective_id=0, has_side_effects=True
        ),
        name="front",
    )(
        cell_index.reshape(1, parts),
        cell_tile,
        part_feat,
        mesh_state.reshape(cells, channels),
        part_feat,
        pairs,
        w_enc,
        w_pair,
        w_edge,
    )

    one_plane = lambda f: pl.BlockSpec((plane, channels), f)
    by_layer = pl.BlockSpec((planes * cz, channels), lambda g: (g, 0))
    by_speed = pl.BlockSpec((3, members), lambda g: (0, g))
    mesh2, stay_feat, vel1, packed, totals = pl.pallas_call(
        functools.partial(node_kernel, plane, cz, cap),
        grid=(count,),
        out_shape=(
            jax.ShapeDtypeStruct((cells, channels), bf16),
            jax.ShapeDtypeStruct((parts, width), bf16),
            jax.ShapeDtypeStruct((3, parts), f32),
            jax.ShapeDtypeStruct((8, cap + 16, width), bf16),
            jax.ShapeDtypeStruct((4, LANES), f32),
        ),
        in_specs=[
            one_plane(lambda g: (jnp.maximum(g * planes - 1, 0), 0)),
            by_cells,
            one_plane(lambda g: (jnp.minimum(g * planes + planes, cx - 1), 0)),
            whole((plane, channels)),
            whole((plane, channels)),
            by_layer,
            by_layer,
            by_tile,
            by_tile,
            by_row,
            by_rows,
            by_rows,
            by_row,
            by_speed,
            whole(w_mesh.shape),
            whole(w_node.shape),
            whole(w_accel.shape),
        ],
        out_specs=(
            by_cells,
            by_rows,
            by_speed,
            whole((8, cap + 16, width)),
            whole((4, LANES)),
        ),
        scratch_shapes=[
            pltpu.VMEM((8 * cap, width + LANES), bf16),
            pltpu.VMEM((8, LANES), f32),
            pltpu.VMEM((2 * LANES, 2 * LANES), bf16),
            pltpu.VMEM((2 * width, 2 * width), bf16),
            pltpu.VMEM(w_node.shape, bf16),
            pltpu.VMEM((LANES, LANES), bf16),
        ],
        compiler_params=params,
        name="nodes",
    )(
        mesh1,
        mesh1,
        mesh1,
        xlo,
        xhi,
        ylo,
        yhi,
        cell_tile,
        dest_tile,
        dest_row,
        edge_sum,
        part_feat,
        mass_row,
        velocity,
        w_mesh,
        w_node,
        w_accel,
    )

    inside = pl.BlockSpec(memory_space=pltpu.VMEM)
    dma = lambda n: pltpu.SemaphoreType.DMA((n,))
    arrived_feat, arrived_vel, stay_vel = pl.pallas_call(
        functools.partial(tail_kernel, nx, ny, cap),
        out_shape=(
            jax.ShapeDtypeStruct((8 * cap, width), bf16),
            jax.ShapeDtypeStruct((4, 8 * cap), f32),
            jax.ShapeDtypeStruct((3, parts), f32),
        ),
        in_specs=[inside] * 4,
        out_specs=(anywhere, inside, inside),
        scratch_shapes=[
            pltpu.VMEM((nx, 4, LANES), f32),
            pltpu.VMEM((4, LANES), f32),
            pltpu.VMEM((ny, 4, LANES), f32),
            pltpu.VMEM((8, 16, LANES), bf16),
            dma(nx - 1),
            dma(nx - 1),
            dma(ny - 1),
            dma(ny - 1),
            dma(8),
            dma(8),
            dma(8),
            dma(8),
        ],
        compiler_params=pltpu.CompilerParams(
            vmem_limit_bytes=16 * 1024 * 1024, collective_id=1, has_side_effects=True
        ),
        name="tail",
    )(packed, totals, vel1, dest_row)
    return (mesh2.reshape(shape), stay_feat, stay_vel, arrived_feat, arrived_vel)


def solution(mesh):
    placed = (
        P("gx", "gy", None, None),
        P(("gx", "gy"), None),
        P(("gx", "gy")),
        P(None, ("gx", "gy")),
        P(("gx", "gy")),
        P(("gx", "gy")),
        P(None, ("gx", "gy")),
        P(),
        P(),
        P(),
        P(),
        P(),
        P(),
    )
    return jax.shard_map(
        shards,
        mesh=mesh,
        in_specs=placed,
        out_specs=(
            P("gx", "gy", None, None),
            P(("gx", "gy"), None),
            P(None, ("gx", "gy")),
            P(("gx", "gy"), None),
            P(None, ("gx", "gy")),
        ),
        check_vma=False,
    )
```

time: 79.4 us -> 68.7 us (0.87)
  Pallas kernels: 72.6 us -> 63.3 us
  local copies, waits for them, and re-layouts: 5.68 us -> 4.42 us
    pallas_call x1, Pallas kernels: 27.4 us -> 21.2 us  [shards(): pl.pallas_call(functools.partial(node_kernel, plane, cz, cap), grid=(coun...]
    pallas_call x1, Pallas kernels: 31.2 us -> 28.5 us  [shards(): pl.pallas_call(functools.partial(front_kernel, turns, plane, cz, CHUNK),...]
    pad x1 -> x0, local copies, waits for them, and re-layouts: 1.26 us -> none  [shards(): accel8 = jnp.pad(w_accel, ((0, 8 - w_accel.shape[0]), (0, 0)))]
where the time goes in v2:
time: 68.7 us; the launch traced here: 68.4 us
  Pallas kernels  63.3 us (92%)
  local copies, waits for them, and re-layouts  4.42 us (6%)
    pallas_call x1, Pallas kernels, shards(): pl.pallas_call(functools.partial(front_kernel, turns, plane, cz, CHUNK),...  28.5 us
    pallas_call x1, Pallas kernels, shards(): pl.pallas_call(functools.partial(node_kernel, plane, cz, cap), grid=(coun...  21.2 us
    pallas_call x1, Pallas kernels, shards(): pl.pallas_call(functools.partial(tail_kernel, nx, ny, cap), out_shape=(ja...  13.6 us
    unnamed x11, local copies, waits for them, and re-layouts  4.42 us

profile of v2, /device:TPU:0, one launch (start us, length us, event | category | flops | bytes accessed | tf_op | source)
XLA Modules:
  0.0 68.4 jit_solution(9037342279192893123)
XLA Ops:
  0.6 28.5 %front.1 = (bf16[16384,128]{1,0:T(8,128)(2,1)}, bf16[4096,128]{1,0:T(8,128)(2,1)}, bf16[1024,128]{1,0:T(8,128)(2,1)}, bf16[1024,128]{1,0:T(8,128)(2,1)}, bf16[51...) custom-call(s32[1,4096]{1,0:T(1,128)} %bitcast.11, s32[8,4,128]{2,1,0:T(4,128)} %bitcast.12, bf16[4096,128]{1,0:T(8,128)(2,1)} %feat_ref.3, ...), custom_call_target="tpu_custom_call" | custom-call | tf_op jit(solution)/shard_map/front/pallas_call | solution.py:513
  29.2 0.0 copy-start.1
  29.2 21.2 %nodes.1 = (bf16[16384,128]{1,0:T(8,128)(2,1)}, bf16[4096,128]{1,0:T(8,128)(2,1)}, f32[3,4096]{1,0:T(4,128)}, bf16[8,144,128]{2,1,0:T(8,128)(2,1)}, f32[4,128]{1,0:T(4,128)}) custom-call(bf16[16384,128]{1,0:T(8,128)(2,1)} %get-tuple-element.19.below_ref.centre_ref.above_ref, bf16[16384,128]{1,0:T(8,128)(2,1)} %get-tuple-element.19.below_ref.centre_ref.above_ref, ...), custom_call_target="tpu_custom_call" | custom-call | tf_op jit(solution)/shard_map/nodes/pallas_call | solution.py:569
  50.4 0.0 copy-done.1
  50.4 0.0 copy-start
  50.4 1.0 %copy-done = bf16[8,144,128]{2,1,0:T(8,128)(2,1)S(1)} copy-done((bf16[8,144,128]{2,1,0:T(8,128)(2,1)S(1)}, bf16[8,144,128]{2,1,0:T(8,128)(2,1)}, u32[]{:S(2)}) %copy-start) | copy-done | bytes 294936
  51.3 0.0 copy-start.2
  51.3 0.8 %copy-done.2 = f32[3,4096]{1,0:T(4,128)S(1)} copy-done((f32[3,4096]{1,0:T(4,128)S(1)}, f32[3,4096]{1,0:T(4,128)}, u32[]{:S(2)}) %copy-start.2) | copy-done | bytes 49176
  52.2 0.0 copy-start.3
  52.2 0.7 copy-done.3
  52.9 13.6 %tail.1 = (bf16[1024,128]{1,0:T(8,128)(2,1)S(1)}, f32[4,1024]{1,0:T(4,128)S(1)}, f32[3,4096]{1,0:T(4,128)S(1)}) custom-call(bf16[8,144,128]{2,1,0:T(8,128)(2,1)S(1)} %copy-done, f32[4,128]{1,0:T(4,128)S(1)} %copy-done.3, f32[3,4096]{1,0:T(4,128)S(1)} %copy-done.2, s32[1,4096]{1,0:T(1,128)S(1)} %bitcast.9), custom_call_target="tpu_custom_call" | custom-call | tf_op jit(solution)/shard_map/tail/pallas_call | solution.py:637
  66.4 0.6 copy.21
  67.1 0.7 %copy.22 = bf16[1024,128]{1,0:T(8,128)(2,1)} copy(bf16[1024,128]{1,0:T(8,128)(2,1)S(1)} %get-tuple-element.41) | data formatting | bytes 524288
  67.8 0.6 copy.23
Async XLA Ops:
  29.2 21.2 %copy-start.1 = (s32[4096]{0:T(1024)S(1)}, s32[4096]{0:T(1024)}, u32[]{:S(2)}) copy-start(s32[4096]{0:T(1024)} %param.17) | copy-start | bytes 49156
  50.4 1.0 %copy-start = (bf16[8,144,128]{2,1,0:T(8,128)(2,1)S(1)}, bf16[8,144,128]{2,1,0:T(8,128)(2,1)}, u32[]{:S(2)}) copy-start(bf16[8,144,128]{2,1,0:T(8,128)(2,1)} %get-tuple-element.27.packed_ref) | copy-start | bytes 884740
  51.3 0.8 %copy-start.2 = (f32[3,4096]{1,0:T(4,128)S(1)}, f32[3,4096]{1,0:T(4,128)}, u32[]{:S(2)}) copy-start(f32[3,4096]{1,0:T(4,128)} %get-tuple-element.29.vel1_ref) | copy-start | bytes 147460
  52.2 0.7 copy-start.3

commit v3 on v2

--- a/solution.py
+++ b/solution.py
@@ -8,8 +8,11 @@
 
 directions = ((-1, -1), (-1, 0), (-1, 1), (0, -1), (0, 1), (1, -1), (1, 0), (1, 1))
 LANES = 128
-VMEM_LIMIT = 60 * 1024 * 1024
+VMEM_LIMIT = 28 * 1024 * 1024
 CHUNK = 512
+EDGE_GROUPS = 2
+NODE_GROUPS = 2
+FLIP = True
 MESH = pl.DeviceIdType.MESH
 
 
@@ -21,6 +24,10 @@
 
 def silu_of_twice(half):
     return half + half * jnp.tanh(half)
+
+
+def wide(rows):
+    return rows.astype(jnp.float32)
 
 
 def f32dot(a, b):
@@ -68,9 +75,7 @@
     state_ref,
     feat_ref,
     pairs_ref,
-    w_enc_ref,
-    w_pair_ref,
-    w_edge_ref,
+    w_both_ref,
     mesh1_ref,
     edge_ref,
     xlo_ref,
@@ -85,7 +90,8 @@
 ):
     turn = pl.program_id(0)
     last = pl.num_programs(0) - 1
-    members, width = feat_ref.shape
+    width = feat_ref.shape[1]
+    members = feat_ref.shape[0] // EDGE_GROUPS
     groups = cell_tile_ref.shape[0]
     span = state_ref.shape[0] // groups
     planes = state_ref.shape[0] // plane
@@ -110,13 +116,7 @@
     @pl.when(turn == 0)
     def _():
         greet(beside)
-        half_pair_ref[...] = (0.5 * w_pair_ref[...].astype(jnp.float32)).T.astype(jnp.bfloat16)
-
-    @pl.when(turn == turns)
-    def _():
-        pl.semaphore_wait(pltpu.get_barrier_semaphore(), len(beside))
-        for copy in copies():
-            copy.start()
+        half_pair_ref[...] = (0.5 * w_both_ref[:, width:].astype(jnp.float32)).T.astype(jnp.bfloat16)
 
     @pl.when(turn < turns)
     def _():
@@ -125,7 +125,7 @@
             base = (turn * groups + g) * span
             mine = slice(g * members, (g + 1) * members)
             cols = (cell_tile_ref[g] - base).T
-            grown = f32dot(enc_feat_ref[mine, :], w_enc_ref[...])
+            grown = f32dot(enc_feat_ref[mine, :], w_both_ref[:, :width])
             low, high = [], []
             for j in range(members // LANES):
                 rows = grown[j * LANES : (j + 1) * LANES]
@@ -160,30 +160,44 @@
     def _():
         xsend_ref[0] = mesh1_ref[(planes - 1) * plane :, :]
 
-    base = turn * members
-    table = nt_dot(half_pair_ref[...], feat_ref[...]).astype(jnp.bfloat16)
-    tables = [
-        jnp.concatenate([table[:width, :half], table[:width, half:]], axis=0),
-        jnp.concatenate([table[width:, :half], table[width:, half:]], axis=0),
-    ]
-    total = jnp.zeros((half, 2 * width), jnp.float32)
-    for first in range(0, pairs_ref.shape[1], chunk):
-        pre = None
-        for end in range(2):
-            rows = pairs_ref[end : end + 1, first : first + chunk] - base
-            upper = rows >= half
-            hot = down_hot(jnp.where(upper, rows - half, rows), half)
-            got = f32dot(tables[end], hot)
-            picked = jnp.where(upper, got[width:], got[:width])
-            pre = picked if pre is None else pre + picked
-        act = silu_of_twice(pre).astype(jnp.bfloat16)
-        share = jnp.where(upper, 1.0, 0.0)
-        acts = jnp.concatenate(
-            [act * (1.0 - share).astype(jnp.bfloat16), act * share.astype(jnp.bfloat16)], axis=0
-        )
-        total = total + nt_dot(hot, acts)
-    total = jnp.concatenate([total[:, :width], total[:, width:]], axis=0)
-    edge_ref[...] = f32dot(total.astype(jnp.bfloat16), w_edge_ref[...]).astype(jnp.bfloat16)
+    @pl.when(turn == turns - 1)
+    def _():
+        pl.semaphore_wait(pltpu.get_barrier_semaphore(), len(beside))
+        for copy in copies():
+            copy.start()
+
+    totals = [jnp.zeros((half, 2 * width), jnp.float32)] * EDGE_GROUPS
+    tables = []
+    for g in range(EDGE_GROUPS):
+        table = nt_dot(half_pair_ref[...], feat_ref[g * members : (g + 1) * members, :])
+        table = table.astype(jnp.bfloat16)
+        tables.append(jnp.concatenate([table[:width], table[width:]], axis=1))
+    per_group = pairs_ref.shape[1] // EDGE_GROUPS
+    for first in range(0, per_group, chunk):
+        for g in range(EDGE_GROUPS):
+            base = (turn * EDGE_GROUPS + g) * members
+            start = g * per_group + first
+            senders = pairs_ref[0:1, start : start + chunk] - base
+            receivers = pairs_ref[1:2, start : start + chunk] - base
+            upper = receivers >= half
+            hots = [down_hot(senders, half), down_hot(senders - half, half)]
+            hots += [down_hot(receivers, half), down_hot(receivers - half, half)]
+            hot = hots[2] + hots[3]
+            pre = f32dot(tables[g], jnp.concatenate(hots, axis=0))
+            act = silu_of_twice(pre).astype(jnp.bfloat16)
+            share = jnp.where(upper, 1.0, 0.0)
+            acts = jnp.concatenate(
+                [act * (1.0 - share).astype(jnp.bfloat16), act * share.astype(jnp.bfloat16)],
+                axis=0,
+            )
+            if FLIP:
+                totals[g] = totals[g] + nt_dot(acts, hot)
+            else:
+                totals[g] = totals[g] + nt_dot(hot, acts)
+    for g in range(EDGE_GROUPS):
+        total = totals[g].T if FLIP else totals[g]
+        total = jnp.concatenate([total[:, :width], total[:, width:]], axis=0)
+        edge_ref[g * members : (g + 1) * members, :] = total.astype(jnp.bfloat16)
 
     @pl.when(turn == last)
     def _():
@@ -210,6 +224,7 @@
     mass_ref,
     vel_ref,
     w_mesh_ref,
+    w_edge_ref,
     w_node_ref,
     w_accel_ref,
     mesh_ref,
@@ -223,13 +238,14 @@
     wide_w_ref,
     node_w_ref,
     before_ref,
+    push_w_ref,
 ):
     step = pl.program_id(0)
     last = pl.num_programs(0) - 1
-    span, width = centre_ref.shape
-    members = feat_ref.shape[0]
-    planes = span // plane
-    base = step * span
+    width = centre_ref.shape[1]
+    span = centre_ref.shape[0] // NODE_GROUPS
+    members = feat_ref.shape[0] // NODE_GROUPS
+    planes = centre_ref.shape[0] // plane
     block = 2 * LANES
 
     @pl.when(step == 0)
@@ -254,15 +270,16 @@
             axis=0,
         ).astype(jnp.bfloat16)
         node_w_ref[...] = (0.5 * w_node_ref[...].astype(jnp.float32)).astype(jnp.bfloat16)
+        push = jnp.concatenate(
+            [wide(w_accel_ref[...]), jnp.zeros((LANES - 3, width), jnp.float32)], axis=0
+        )
+        push_w_ref[...] = push.T.astype(jnp.bfloat16)
         before_ref[...] = jnp.where(
             lax.broadcasted_iota(jnp.int32, (LANES, LANES), 0)
             < lax.broadcasted_iota(jnp.int32, (LANES, LANES), 1),
             1.0,
             0.0,
         ).astype(jnp.bfloat16)
-
-    def wide(rows):
-        return rows.astype(jnp.float32)
 
     for p in range(planes):
         for pair in range(0, plane, 2 * block):
@@ -308,60 +325,90 @@
 
     turns = members // LANES
     top = span // 2
-    cell_cols = (cell_ref[0] - base).T
-    dest_cols = dest_ref[0].T
-    hots, uppers = [], []
-    for j in range(turns):
-        col = cell_cols[:, j : j + 1]
-        upper = col >= top
-        uppers.append(upper)
-        hots.append(over_hot(jnp.where(upper, col - top, col), top))
-    pair = jnp.concatenate([mesh_ref[:top, :], mesh_ref[top:, :]], axis=1)
-    found = f32dot(jnp.concatenate(hots, axis=0), pair)
-    near = jnp.concatenate(
-        [
-            jnp.where(
-                uppers[j],
-                found[j * LANES : (j + 1) * LANES, width:],
-                found[j * LANES : (j + 1) * LANES, :width],
+    some = 2 * LANES
+    items = [(g, start) for start in range(0, members, some) for g in range(NODE_GROUPS)]
+    pairs, cell_cols, dest_cols = [], [], []
+    for g in range(NODE_GROUPS):
+        cells = g * span
+        pairs.append(
+            jnp.concatenate(
+                [mesh_ref[cells : cells + top, :], mesh_ref[cells + top : cells + span, :]], axis=1
             )
-            for j in range(turns)
-        ],
-        axis=0,
-    ).astype(jnp.bfloat16)
-    update = f32dot(jnp.concatenate([edge_ref[...], near], axis=1), node_w_ref[...])
-    h_new = (wide(feat_ref[...]) + silu_of_twice(update)).astype(jnp.bfloat16)
-    h_wide = h_new.astype(jnp.float32)
-    for j in range(turns):
-        rows = slice(j * LANES, (j + 1) * LANES)
-        stay_ref[rows, :] = jnp.where(dest_cols[:, j : j + 1] == 0, h_wide[rows], 0.0).astype(
-            jnp.bfloat16
         )
-    vel1 = vel_ref[...] + nt_dot(w_accel_ref[...], h_new)
-    mass = mass_ref[...]
-    vel1_ref[...] = vel1
-    sums = jnp.concatenate([mass * vel1, mass], axis=0)
-    total_ref[...] += sum(sums[:, j * LANES : (j + 1) * LANES] for j in range(turns))
-
-    dest = dest_row_ref[...]
-    ways = lax.broadcasted_iota(jnp.int32, (8, members), 0) + 1
-    chosen = jnp.where(ways == dest, 1.0, 0.0)
-    stacked = jnp.concatenate([chosen[:, j * LANES : (j + 1) * LANES] for j in range(turns)], axis=0)
-    earlier = f32dot(stacked.astype(jnp.bfloat16), before_ref[...])
-    counts = jnp.sum(stacked, axis=1, keepdims=True)
+        cell_cols.append((cell_ref[g] - (step * NODE_GROUPS + g) * span).T)
+        dest_cols.append(dest_ref[g].T)
+    nears = {}
+    for g, start in items:
+        hots, uppers = [], []
+        for j in range(start // LANES, (start + some) // LANES):
+            col = cell_cols[g][:, j : j + 1]
+            upper = col >= top
+            uppers.append(upper)
+            hots.append(over_hot(jnp.where(upper, col - top, col), top))
+        found = f32dot(jnp.concatenate(hots, axis=0), pairs[g])
+        nears[g, start] = jnp.concatenate(
+            [
+                jnp.where(
+                    upper,
+                    found[j * LANES : (j + 1) * LANES, width:],
+                    found[j * LANES : (j + 1) * LANES, :width],
+                )
+                for j, upper in enumerate(uppers)
+            ],
+            axis=0,
+        ).astype(jnp.bfloat16)
+    parts = {}
+    for g, start in items:
+        rows = slice(g * members + start, g * members + start + some)
+        edge_sum = f32dot(edge_ref[rows, :], w_edge_ref[...]).astype(jnp.bfloat16)
+        update = f32dot(jnp.concatenate([edge_sum, nears[g, start]], axis=1), node_w_ref[...])
+        parts[g, start] = (wide(feat_ref[rows, :]) + silu_of_twice(update)).astype(jnp.bfloat16)
+    pushed = {item: f32dot(parts[item], push_w_ref[...]) for item in items}
     done = carry_ref[:, :1]
-    places = []
-    for j in range(turns):
-        rows = slice(8 * j, 8 * (j + 1))
-        places.append(jnp.where(stacked[rows] > 0, earlier[rows] + done, -1.0))
-        done = done + counts[rows]
+    all_values, all_places = [], []
+    for g in range(NODE_GROUPS):
+        mine = slice(g * members, (g + 1) * members)
+        starts = range(0, members, some)
+        h_new = jnp.concatenate([parts[g, start] for start in starts], axis=0)
+        mass = mass_ref[:, mine]
+        extra = jnp.concatenate(
+            [vel_ref[:, mine], mass, jnp.zeros((LANES - 4, members), jnp.float32)], axis=0
+        )
+        extra = extra.T + jnp.concatenate([pushed[g, start] for start in starts], axis=0)
+        all_values.append(jnp.concatenate([h_new, extra.astype(jnp.bfloat16)], axis=1))
+
+        dest = dest_row_ref[:, mine]
+        ways = lax.broadcasted_iota(jnp.int32, (8, members), 0) + 1
+        chosen = jnp.where(ways == dest, 1.0, 0.0)
+        stacked = jnp.concatenate(
+            [chosen[:, j * LANES : (j + 1) * LANES] for j in range(turns)], axis=0
+        )
+        earlier = f32dot(stacked.astype(jnp.bfloat16), before_ref[...])
+        counts = jnp.sum(stacked, axis=1, keepdims=True)
+        places = []
+        for j in range(turns):
+            rows = slice(8 * j, 8 * (j + 1))
+            places.append(jnp.where(stacked[rows] > 0, earlier[rows] + done, -1.0))
+            done = done + counts[rows]
+        all_places.append(jnp.concatenate(places, axis=1))
     carry_ref[...] = jnp.broadcast_to(done, carry_ref.shape)
-    place = jnp.concatenate(places, axis=1)
-    extra = jnp.concatenate([vel1, mass, jnp.zeros((LANES - 4, members), jnp.float32)], axis=0)
-    values = jnp.concatenate([h_new, extra.T.astype(jnp.bfloat16)], axis=1)
+    values = jnp.concatenate(all_values, axis=0)
+    place = jnp.concatenate(all_places, axis=1)
     for k in range(8):
         rows = slice(k * cap, (k + 1) * cap)
         slots_ref[rows, :] += f32dot(down_hot(place[k : k + 1], cap), values).astype(jnp.bfloat16)
+    for g in range(NODE_GROUPS):
+        mine = slice(g * members, (g + 1) * members)
+        mass = mass_ref[:, mine]
+        vel1 = vel_ref[:, mine] + nt_dot(w_accel_ref[...], all_values[g][:, :width])
+        vel1_ref[:, mine] = vel1
+        sums = jnp.concatenate([mass * vel1, mass], axis=0)
+        total_ref[...] += sum(sums[:, j * LANES : (j + 1) * LANES] for j in range(turns))
+        for j in range(turns):
+            rows = slice(j * LANES, (j + 1) * LANES)
+            stay_ref[g * members + j * LANES : g * members + (j + 1) * LANES, :] = jnp.where(
+                dest_cols[g][:, j : j + 1] == 0, wide(all_values[g][rows, :width]), 0.0
+            ).astype(jnp.bfloat16)
 
     @pl.when(step == last)
     def _():
@@ -382,13 +429,18 @@
     nx,
     ny,
     cap,
+    packed_hbm,
+    totals_hbm,
+    vel1_hbm,
+    dest_hbm,
+    feat_ref,
+    arrived_ref,
+    stay_ref,
     packed_ref,
     totals_ref,
     vel1_ref,
     dest_ref,
-    feat_ref,
-    arrived_ref,
-    stay_ref,
+    load_sems,
     xsum_ref,
     part_ref,
     ysum_ref,
@@ -405,6 +457,20 @@
     me_x, me_y = lax.axis_index("gx"), lax.axis_index("gy")
     places = meeting_places(nx, ny)
     greet(places)
+    loads = [
+        pltpu.make_async_copy(source, target, load_sems.at[n])
+        for n, (source, target) in enumerate(
+            (
+                (totals_hbm, totals_ref),
+                (packed_hbm, packed_ref),
+                (vel1_hbm, vel1_ref),
+                (dest_hbm, dest_ref),
+            )
+        )
+    ]
+    for load in loads:
+        load.start()
+    loads[0].wait()
     xsum_ref[me_x] = totals_ref[...]
     pl.semaphore_wait(pltpu.get_barrier_semaphore(), len(places))
 
@@ -423,6 +489,7 @@
     along_x = [
         copy(totals_ref, xsum_ref.at[me_x], send_x, recv_x, o - 1, o, 0) for o in range(1, nx)
     ]
+    loads[1].wait()
     moving = [
         copy(packed_ref.at[k, pl.ds(cap, 16)], got_ref.at[k], send_m, recv_m, k, dx, dy)
         for k, (dx, dy) in enumerate(directions)
@@ -451,6 +518,8 @@
         made.wait()
     sums = jnp.sum(jnp.sum(ysum_ref[...], axis=0), axis=1, keepdims=True)
     drift = sums[:3] / sums[3:4]
+    loads[2].wait()
+    loads[3].wait()
     stay_ref[...] = jnp.where(dest_ref[...] == 0, vel1_ref[...] - drift, 0.0)
     for made in moving:
         made.wait()
@@ -506,13 +575,14 @@
     dest_tile = dest.reshape(count, members // LANES, LANES)
     mass_row = mass.reshape(1, parts)
 
-    groups = 2
+    w_both = jnp.concatenate([w_enc, w_pair], axis=1)
+    groups = 2 * EDGE_GROUPS
     turns = count // groups
     early = lambda g: jnp.minimum(g, turns - 1)
     anywhere = pl.BlockSpec(memory_space=pl.ANY)
     mesh1, edge_sum, xlo, xhi, ylo, yhi = pl.pallas_call(
         functools.partial(front_kernel, turns, plane, cz, CHUNK),
-        grid=(count,),
+        grid=(count // EDGE_GROUPS,),
         out_shape=(
             jax.ShapeDtypeStruct((cells, channels), bf16),
             jax.ShapeDtypeStruct((parts, width), bf16),
@@ -526,15 +596,13 @@
             pl.BlockSpec((groups, members // LANES, LANES), lambda g: (early(g), 0, 0)),
             pl.BlockSpec((groups * members, width), lambda g: (early(g), 0)),
             pl.BlockSpec((groups * span, channels), lambda g: (early(g), 0)),
-            by_rows,
-            pl.BlockSpec((2, per_group), lambda g: (0, g)),
-            whole(w_enc.shape),
-            whole(w_pair.shape),
-            whole(w_edge.shape),
+            pl.BlockSpec((EDGE_GROUPS * members, width), lambda g: (g, 0)),
+            pl.BlockSpec((2, EDGE_GROUPS * per_group), lambda g: (0, g)),
+            whole(w_both.shape),
         ],
         out_specs=(
             pl.BlockSpec((groups * span, channels), lambda g: (early(g), 0)),
-            by_rows,
+            pl.BlockSpec((EDGE_GROUPS * members, width), lambda g: (g, 0)),
             anywhere,
             anywhere,
             anywhere,
@@ -558,17 +626,21 @@
         mesh_state.reshape(cells, channels),
         part_feat,
         pairs,
-        w_enc,
-        w_pair,
-        w_edge,
+        w_both,
     )
 
+    many = NODE_GROUPS
+    by_rows = pl.BlockSpec((many * members, width), lambda g: (g, 0))
+    by_cells = pl.BlockSpec((many * span, channels), lambda g: (g, 0))
+    by_row = pl.BlockSpec((1, many * members), lambda g: (0, g))
+    by_tile = pl.BlockSpec((many, members // LANES, LANES), lambda g: (g, 0, 0))
+    planes = many * (span // plane)
     one_plane = lambda f: pl.BlockSpec((plane, channels), f)
     by_layer = pl.BlockSpec((planes * cz, channels), lambda g: (g, 0))
-    by_speed = pl.BlockSpec((3, members), lambda g: (0, g))
+    by_speed = pl.BlockSpec((3, many * members), lambda g: (0, g))
     mesh2, stay_feat, vel1, packed, totals = pl.pallas_call(
         functools.partial(node_kernel, plane, cz, cap),
-        grid=(count,),
+        grid=(count // many,),
         out_shape=(
             jax.ShapeDtypeStruct((cells, channels), bf16),
             jax.ShapeDtypeStruct((parts, width), bf16),
@@ -592,6 +664,7 @@
             by_row,
             by_speed,
             whole(w_mesh.shape),
+            whole(w_edge.shape),
             whole(w_node.shape),
             whole(w_accel.shape),
         ],
@@ -609,6 +682,7 @@
             pltpu.VMEM((2 * width, 2 * width), bf16),
             pltpu.VMEM(w_node.shape, bf16),
             pltpu.VMEM((LANES, LANES), bf16),
+            pltpu.VMEM((width, LANES), bf16),
         ],
         compiler_params=params,
         name="nodes",
@@ -628,6 +702,7 @@
         mass_row,
         velocity,
         w_mesh,
+        w_edge,
         w_node,
         w_accel,
     )
@@ -641,9 +716,14 @@
             jax.ShapeDtypeStruct((4, 8 * cap), f32),
             jax.ShapeDtypeStruct((3, parts), f32),
         ),
-        in_specs=[inside] * 4,
+        in_specs=[pl.BlockSpec(memory_space=pltpu.HBM)] * 4,
         out_specs=(anywhere, inside, inside),
         scratch_shapes=[
+            pltpu.VMEM(packed.shape, bf16),
+            pltpu.VMEM(totals.shape, f32),
+            pltpu.VMEM(vel1.shape, f32),
+            pltpu.VMEM(dest_row.shape, jnp.int32),
+            dma(4),
             pltpu.VMEM((nx, 4, LANES), f32),
             pltpu.VMEM((4, LANES), f32),
             pltpu.VMEM((ny, 4, LANES), f32),

time: 68.7 us -> 53.7 us (0.78)
  Pallas kernels: 63.3 us -> 44.6 us
  local copies, waits for them, and re-layouts: 4.42 us -> 7.02 us
  other arithmetic: 0 us -> 0.92 us
    pallas_call x1, Pallas kernels: 28.5 us -> 18.4 us  [shards(): pl.pallas_call(functools.partial(front_kernel, turns, plane, cz, CHUNK),...]
    pallas_call x1, Pallas kernels: 21.2 us -> 13.1 us  [shards(): pl.pallas_call(functools.partial(node_kernel, plane, cz, cap), grid=(coun...]
    unnamed x11 -> x25, local copies, waits for them, and re-layouts: 4.42 us -> 7.02 us
    concatenate x0 -> x1, other arithmetic: none -> 0.92 us  [shards(): w_both = jnp.concatenate([w_enc, w_pair], axis=1)]
where the time goes in v3:
time: 53.7 us; the launch traced here: 53.3 us
  Pallas kernels  44.6 us (83%)
  local copies, waits for them, and re-layouts  7.02 us (13%)
  other arithmetic  0.92 us (2%)
  between operations  0.77 us (1%)
    pallas_call x1, Pallas kernels, shards(): pl.pallas_call(functools.partial(front_kernel, turns, plane, cz, CHUNK),...  18.4 us
    pallas_call x1, Pallas kernels, shards(): pl.pallas_call(functools.partial(tail_kernel, nx, ny, cap), out_shape=(ja...  13.2 us
    pallas_call x1, Pallas kernels, shards(): pl.pallas_call(functools.partial(node_kernel, plane, cz, cap), grid=(coun...  13.1 us
    unnamed x25, local copies, waits for them, and re-layouts  7.02 us

profile of v3, /device:TPU:0, one launch (start us, length us, event | category | flops | bytes accessed | tf_op | source)
XLA Modules:
  0.0 53.3 jit_solution(10333065611279898588)
XLA Ops:
  0.6 0.0 copy-start.4
  0.6 0.0 copy-start.10
  0.7 0.0 copy-start.6
  0.7 0.0 copy-start.7
  0.7 0.0 copy-start.5
  0.7 0.0 copy-start.9
  0.7 0.9 %pad_maximum_fusion.w_both_ref = bf16[128,384]{1,0:T(8,128)(2,1)S(1)} fusion(bf16[128,256]{1,0:T(8,128)(2,1)} %param.22, bf16[128,128]{1,0:T(8,128)(2,1)} %param.20), kind=kLoop, calls=%fused_computation | loop fusion | flops 196608 | bytes 196608 | tf_op jit(solution)/shard_map/concatenate | solution.py:578
  1.6 0.0 copy-start
  1.6 1.2 %copy-done = bf16[4096,128]{1,0:T(8,128)(2,1)S(1)} copy-done((bf16[4096,128]{1,0:T(8,128)(2,1)S(1)}, bf16[4096,128]{1,0:T(8,128)(2,1)}, u32[]{:S(2)}) %copy-start) | copy-done | bytes 1048600
  2.8 2.2 %copy-done.1 = bf16[16,32,32,128]{3,2,1,0:T(8,128)(2,1)S(1)} copy-done((bf16[16,32,32,128]{3,2,1,0:T(8,128)(2,1)S(1)}, bf16[16,32,32,128]{3,2,1,0:T(8,128)(2,1)}, u32[]{:S(2)}) %copy-start.1) | copy-done | bytes 4194328
  5.0 0.9 %copy-done.2 = s32[2,24576]{1,0:T(2,128)S(1)} copy-done((s32[2,24576]{1,0:T(2,128)S(1)}, s32[2,24576]{1,0:T(2,128)}, u32[]{:S(2)}) %copy-start.2) | copy-done | bytes 196632
  6.0 0.7 %copy-done.3 = s32[4096]{0:T(1024)S(1)} copy-done((s32[4096]{0:T(1024)S(1)}, s32[4096]{0:T(1024)}, u32[]{:S(2)}) %copy-start.3) | copy-done | bytes 16408
  6.7 18.4 %front.1 = (bf16[16384,128]{1,0:T(8,128)(2,1)S(1)}, bf16[4096,128]{1,0:T(8,128)(2,1)S(1)}, bf16[1024,128]{1,0:T(8,128)(2,1)S(1)}, bf16[1024,128]{1,0:T(8,128)(2,...) custom-call(s32[1,4096]{1,0:T(1,128)S(1)} %bitcast.8, s32[8,4,128]{2,1,0:T(4,128)S(1)} %bitcast.9, ...), custom_call_target="tpu_custom_call" | custom-call | tf_op jit(solution)/shard_map/front/pallas_call | solution.py:583
  25.1 0.0 copy-done.4
  25.1 0.0 copy-done.10
  25.1 0.0 copy-done.6
  25.1 0.0 copy-done.7
  25.1 0.0 copy-done.5
  25.1 0.0 copy-done.9
  25.2 13.1 %nodes.1 = (bf16[16384,128]{1,0:T(8,128)(2,1)}, bf16[4096,128]{1,0:T(8,128)(2,1)}, f32[3,4096]{1,0:T(4,128)S(1)}, bf16[8,144,128]{2,1,0:T(8,128)(2,1)S(1)}, f32[4,128]{1,0:T(4,128)S(1)}) custom-call(bf16[16384,128]{1,0:T(8,128)(2,1)S(1)} %get-tuple-element.19.below_ref.centre_ref.above_ref, ...), custom_call_target="tpu_custom_call" | custom-call | tf_op jit(solution)/shard_map/nodes/pallas_call | solution.py:641
  38.2 13.2 %tail.1 = (bf16[1024,128]{1,0:T(8,128)(2,1)S(1)}, f32[4,1024]{1,0:T(4,128)S(1)}, f32[3,4096]{1,0:T(4,128)S(1)}) custom-call(bf16[8,144,128]{2,1,0:T(8,128)(2,1)S(1)} %get-tuple-element.27.packed_hbm, f32[4,128]{1,0:T(4,128)S(1)} %get-tuple-element.28.totals_hbm, f32[3,4096]{1,0:T(4,128)S(1)} %get-tuple-element.29.vel1_hbm, s32[1,4096]{1,0:T(1,128)S(1)} %bitcast.13), custom_call_target="tpu_custom_call" | custom-call | tf_op jit(solution)/shard_map/tail/pallas_call | solution.py:712
  51.4 0.6 %copy.21 = f32[3,4096]{1,0:T(4,128)} copy(f32[3,4096]{1,0:T(4,128)S(1)} %get-tuple-element.40) | data formatting | bytes 98304
  52.0 0.7 %copy.22 = bf16[1024,128]{1,0:T(8,128)(2,1)} copy(bf16[1024,128]{1,0:T(8,128)(2,1)S(1)} %get-tuple-element.41) | data formatting | bytes 524288
  52.7 0.6 %copy.23 = f32[4,1024]{1,0:T(4,128)} copy(f32[4,1024]{1,0:T(4,128)S(1)} %get-tuple-element.42) | data formatting | bytes 32768
  (5 shorter events, 0.0 us)
Async XLA Ops:
  0.6 24.5 %copy-start.4 = (s32[4096]{0:T(1024)S(1)}, s32[4096]{0:T(1024)}, u32[]{:S(2)}) copy-start(s32[4096]{0:T(1024)} %param.17) | copy-start | bytes 49156
  0.6 24.5 %copy-start.10 = (bf16[3,128]{1,0:T(4,128)(2,1)S(1)}, bf16[3,128]{1,0:T(4,128)(2,1)}, u32[]{:S(2)}) copy-start(bf16[3,128]{1,0:T(4,128)(2,1)} %w_accel_ref.1) | copy-start | bytes 2308
  0.7 24.5 %copy-start.6 = (bf16[256,128]{1,0:T(8,128)(2,1)S(1)}, bf16[256,128]{1,0:T(8,128)(2,1)}, u32[]{:S(2)}) copy-start(bf16[256,128]{1,0:T(8,128)(2,1)} %w_node_ref.1) | copy-start | bytes 196612
  0.7 24.5 %copy-start.7 = (bf16[128,128]{1,0:T(8,128)(2,1)S(1)}, bf16[128,128]{1,0:T(8,128)(2,1)}, u32[]{:S(2)}) copy-start(bf16[128,128]{1,0:T(8,128)(2,1)} %w_mesh_ref.1) | copy-start | bytes 98308
  0.7 24.5 %copy-start.5 = (f32[3,4096]{1,0:T(4,128)S(1)}, f32[3,4096]{1,0:T(4,128)}, u32[]{:S(2)}) copy-start(f32[3,4096]{1,0:T(4,128)} %vel_ref.1) | copy-start | bytes 147460
  0.7 24.5 %copy-start.9 = (f32[4096]{0:T(1024)S(1)}, f32[4096]{0:T(1024)}, u32[]{:S(2)}) copy-start(f32[4096]{0:T(1024)} %param.18) | copy-start | bytes 49156
  1.6 1.2 %copy-start = (bf16[4096,128]{1,0:T(8,128)(2,1)S(1)}, bf16[4096,128]{1,0:T(8,128)(2,1)}, u32[]{:S(2)}) copy-start(bf16[4096,128]{1,0:T(8,128)(2,1)} %feat_ref.3) | copy-start | bytes 3145732
  2.8 2.2 %copy-start.1 = (bf16[16,32,32,128]{3,2,1,0:T(8,128)(2,1)S(1)}, bf16[16,32,32,128]{3,2,1,0:T(8,128)(2,1)}, u32[]{:S(2)}) copy-start(bf16[16,32,32,128]{3,2,1,0:T(8,128)(2,1)} %param.13) | copy-start | bytes 12582916
  5.0 0.9 %copy-start.2 = (s32[2,24576]{1,0:T(2,128)S(1)}, s32[2,24576]{1,0:T(2,128)}, u32[]{:S(2)}) copy-start(s32[2,24576]{1,0:T(2,128)} %pairs_ref.1) | copy-start | bytes 589828
  6.0 0.7 %copy-start.3 = (s32[4096]{0:T(1024)S(1)}, s32[4096]{0:T(1024)}, u32[]{:S(2)}) copy-start(s32[4096]{0:T(1024)} %param.15) | copy-start | bytes 49156
  6.7 18.5 %copy-start.8 = (bf16[128,128]{1,0:T(8,128)(2,1)S(1)}, bf16[128,128]{1,0:T(8,128)(2,1)}, u32[]{:S(2)}) copy-start(bf16[128,128]{1,0:T(8,128)(2,1)} %w_edge_ref.1) | copy-start | bytes 98308

commit v4 on v3

--- a/solution.py
+++ b/solution.py
@@ -10,8 +10,8 @@
 LANES = 128
 VMEM_LIMIT = 28 * 1024 * 1024
 CHUNK = 512
-EDGE_GROUPS = 2
-NODE_GROUPS = 2
+EDGE_GROUPS = 4
+NODE_GROUPS = 4
 FLIP = True
 MESH = pl.DeviceIdType.MESH
 

time: 53.7 us -> 51.8 us (0.965)
  Pallas kernels: 44.6 us -> 42.7 us
    pallas_call x1, Pallas kernels: 18.4 us -> 16.7 us  [shards(): pl.pallas_call(functools.partial(front_kernel, turns, plane, cz, CHUNK),...]
    pallas_call x1, Pallas kernels: 13.1 us -> 12.2 us  [shards(): pl.pallas_call(functools.partial(node_kernel, plane, cz, cap), grid=(coun...]
    pallas_call x1, Pallas kernels: 13.2 us -> 13.9 us  [shards(): pl.pallas_call(functools.partial(tail_kernel, nx, ny, cap), out_shape=(ja...]
where the time goes in v4:
time: 51.8 us; the launch traced here: 51.4 us
  Pallas kernels  42.7 us (82%)
  local copies, waits for them, and re-layouts  7.02 us (14%)
  other arithmetic  0.92 us (2%)
  between operations  0.77 us (1%)
    pallas_call x1, Pallas kernels, shards(): pl.pallas_call(functools.partial(front_kernel, turns, plane, cz, CHUNK),...  16.7 us
    pallas_call x1, Pallas kernels, shards(): pl.pallas_call(functools.partial(tail_kernel, nx, ny, cap), out_shape=(ja...  13.9 us
    pallas_call x1, Pallas kernels, shards(): pl.pallas_call(functools.partial(node_kernel, plane, cz, cap), grid=(coun...  12.2 us
    unnamed x25, local copies, waits for them, and re-layouts  7.02 us

profile of v4, /device:TPU:0, one launch (start us, length us, event | category | flops | bytes accessed | tf_op | source)
XLA Modules:
  0.0 51.4 jit_solution(12900501826633640961)
XLA Ops:
  0.6 0.0 copy-start.4
  0.6 0.0 copy-start.10
  0.7 0.0 copy-start.6
  0.7 0.0 copy-start.7
  0.7 0.0 copy-start.5
  0.7 0.0 copy-start.9
  0.7 0.9 %pad_maximum_fusion.w_both_ref = bf16[128,384]{1,0:T(8,128)(2,1)S(1)} fusion(bf16[128,256]{1,0:T(8,128)(2,1)} %param.22, bf16[128,128]{1,0:T(8,128)(2,1)} %param.20), kind=kLoop, calls=%fused_computation | loop fusion | flops 196608 | bytes 196608 | tf_op jit(solution)/shard_map/concatenate | solution.py:578
  1.6 0.0 copy-start
  1.6 1.2 %copy-done = bf16[4096,128]{1,0:T(8,128)(2,1)S(1)} copy-done((bf16[4096,128]{1,0:T(8,128)(2,1)S(1)}, bf16[4096,128]{1,0:T(8,128)(2,1)}, u32[]{:S(2)}) %copy-start) | copy-done | bytes 1048600
  2.8 2.2 %copy-done.1 = bf16[16,32,32,128]{3,2,1,0:T(8,128)(2,1)S(1)} copy-done((bf16[16,32,32,128]{3,2,1,0:T(8,128)(2,1)S(1)}, bf16[16,32,32,128]{3,2,1,0:T(8,128)(2,1)}, u32[]{:S(2)}) %copy-start.1) | copy-done | bytes 4194328
  5.0 0.9 %copy-done.2 = s32[2,24576]{1,0:T(2,128)S(1)} copy-done((s32[2,24576]{1,0:T(2,128)S(1)}, s32[2,24576]{1,0:T(2,128)}, u32[]{:S(2)}) %copy-start.2) | copy-done | bytes 196632
  6.0 0.7 %copy-done.3 = s32[4096]{0:T(1024)S(1)} copy-done((s32[4096]{0:T(1024)S(1)}, s32[4096]{0:T(1024)}, u32[]{:S(2)}) %copy-start.3) | copy-done | bytes 16408
  6.7 16.7 %front.1 = (bf16[16384,128]{1,0:T(8,128)(2,1)S(1)}, bf16[4096,128]{1,0:T(8,128)(2,1)S(1)}, bf16[1024,128]{1,0:T(8,128)(2,1)S(1)}, bf16[1024,128]{1,0:T(8,128)(2,...) custom-call(s32[1,4096]{1,0:T(1,128)S(1)} %bitcast.8, s32[8,4,128]{2,1,0:T(4,128)S(1)} %bitcast.9, ...), custom_call_target="tpu_custom_call" | custom-call | tf_op jit(solution)/shard_map/front/pallas_call | solution.py:583
  23.4 0.0 copy-done.4
  23.4 0.0 copy-done.10
  23.4 0.0 copy-done.6
  23.4 0.0 copy-done.7
  23.4 0.0 copy-done.5
  23.4 0.0 copy-done.9
  23.4 12.2 %nodes.1 = (bf16[16384,128]{1,0:T(8,128)(2,1)}, bf16[4096,128]{1,0:T(8,128)(2,1)}, f32[3,4096]{1,0:T(4,128)S(1)}, bf16[8,144,128]{2,1,0:T(8,128)(2,1)S(1)}, f32[4,128]{1,0:T(4,128)S(1)}) custom-call(bf16[16384,128]{1,0:T(8,128)(2,1)S(1)} %get-tuple-element.19.below_ref.centre_ref.above_ref, ...), custom_call_target="tpu_custom_call" | custom-call | tf_op jit(solution)/shard_map/nodes/pallas_call | solution.py:641
  35.6 13.9 %tail.1 = (bf16[1024,128]{1,0:T(8,128)(2,1)S(1)}, f32[4,1024]{1,0:T(4,128)S(1)}, f32[3,4096]{1,0:T(4,128)S(1)}) custom-call(bf16[8,144,128]{2,1,0:T(8,128)(2,1)S(1)} %get-tuple-element.27.packed_hbm, f32[4,128]{1,0:T(4,128)S(1)} %get-tuple-element.28.totals_hbm, f32[3,4096]{1,0:T(4,128)S(1)} %get-tuple-element.29.vel1_hbm, s32[1,4096]{1,0:T(1,128)S(1)} %bitcast.13), custom_call_target="tpu_custom_call" | custom-call | tf_op jit(solution)/shard_map/tail/pallas_call | solution.py:712
  49.5 0.6 %copy.21 = f32[3,4096]{1,0:T(4,128)} copy(f32[3,4096]{1,0:T(4,128)S(1)} %get-tuple-element.40) | data formatting | bytes 98304
  50.1 0.7 %copy.22 = bf16[1024,128]{1,0:T(8,128)(2,1)} copy(bf16[1024,128]{1,0:T(8,128)(2,1)S(1)} %get-tuple-element.41) | data formatting | bytes 524288
  50.8 0.6 %copy.23 = f32[4,1024]{1,0:T(4,128)} copy(f32[4,1024]{1,0:T(4,128)S(1)} %get-tuple-element.42) | data formatting | bytes 32768
  (5 shorter events, 0.0 us)
Async XLA Ops:
  0.6 22.7 %copy-start.4 = (s32[4096]{0:T(1024)S(1)}, s32[4096]{0:T(1024)}, u32[]{:S(2)}) copy-start(s32[4096]{0:T(1024)} %param.17) | copy-start | bytes 49156
  0.6 22.7 %copy-start.10 = (bf16[3,128]{1,0:T(4,128)(2,1)S(1)}, bf16[3,128]{1,0:T(4,128)(2,1)}, u32[]{:S(2)}) copy-start(bf16[3,128]{1,0:T(4,128)(2,1)} %w_accel_ref.1) | copy-start | bytes 2308
  0.7 22.7 %copy-start.6 = (bf16[256,128]{1,0:T(8,128)(2,1)S(1)}, bf16[256,128]{1,0:T(8,128)(2,1)}, u32[]{:S(2)}) copy-start(bf16[256,128]{1,0:T(8,128)(2,1)} %w_node_ref.1) | copy-start | bytes 196612
  0.7 22.7 %copy-start.7 = (bf16[128,128]{1,0:T(8,128)(2,1)S(1)}, bf16[128,128]{1,0:T(8,128)(2,1)}, u32[]{:S(2)}) copy-start(bf16[128,128]{1,0:T(8,128)(2,1)} %w_mesh_ref.1) | copy-start | bytes 98308
  0.7 22.7 %copy-start.5 = (f32[3,4096]{1,0:T(4,128)S(1)}, f32[3,4096]{1,0:T(4,128)}, u32[]{:S(2)}) copy-start(f32[3,4096]{1,0:T(4,128)} %vel_ref.1) | copy-start | bytes 147460
  0.7 22.7 %copy-start.9 = (f32[4096]{0:T(1024)S(1)}, f32[4096]{0:T(1024)}, u32[]{:S(2)}) copy-start(f32[4096]{0:T(1024)} %param.18) | copy-start | bytes 49156
  1.6 1.2 %copy-start = (bf16[4096,128]{1,0:T(8,128)(2,1)S(1)}, bf16[4096,128]{1,0:T(8,128)(2,1)}, u32[]{:S(2)}) copy-start(bf16[4096,128]{1,0:T(8,128)(2,1)} %feat_ref.3) | copy-start | bytes 3145732
  2.8 2.2 %copy-start.1 = (bf16[16,32,32,128]{3,2,1,0:T(8,128)(2,1)S(1)}, bf16[16,32,32,128]{3,2,1,0:T(8,128)(2,1)}, u32[]{:S(2)}) copy-start(bf16[16,32,32,128]{3,2,1,0:T(8,128)(2,1)} %param.13) | copy-start | bytes 12582916
  5.0 0.9 %copy-start.2 = (s32[2,24576]{1,0:T(2,128)S(1)}, s32[2,24576]{1,0:T(2,128)}, u32[]{:S(2)}) copy-start(s32[2,24576]{1,0:T(2,128)} %pairs_ref.1) | copy-start | bytes 589828
  6.0 0.7 %copy-start.3 = (s32[4096]{0:T(1024)S(1)}, s32[4096]{0:T(1024)}, u32[]{:S(2)}) copy-start(s32[4096]{0:T(1024)} %param.15) | copy-start | bytes 49156
  6.7 16.8 %copy-start.8 = (bf16[128,128]{1,0:T(8,128)(2,1)S(1)}, bf16[128,128]{1,0:T(8,128)(2,1)}, u32[]{:S(2)}) copy-start(bf16[128,128]{1,0:T(8,128)(2,1)} %w_edge_ref.1) | copy-start | bytes 98308
